TPU v7x, 256 devices: a whole 4x4x8 slice. The times are simulated.
256 devices in a mesh: pair: 16 (over x_lo, z), aux: 16 (over y, x_hi, core).
Axes of the slice: x: 4 (x_hi: 2, x_lo: 2; x = x_hi * 2 + x_lo), y: 4, z: 8, core: 2. Of those that a mesh axis runs over, the one named last changes fastest.
Arguments:
- panels: bfloat16 [32, 120, 36864], P('pair', None, 'aux'), may hold values from -1 to 1
- amplitudes: bfloat16 [32, 2, 120, 120], P('pair'), may hold values from -0.5 to 0.5
- drive: float32 [32, 2, 14400], P('pair', None, 'aux'), may hold values from -6 to 6
- pno_energy: float32 [32, 120], P('pair'), may hold values from 1 to 3
- occ_energy: float32 [64], replicated, may hold values from -2 to -0.5
- frequency: float32 [1], replicated, may hold values from 0.2 to 2
- pair_lmo: int32 [32, 2], replicated, may hold values from 0 to 63
- neighbours: int32 [32, 8], P('pair'), may hold values from 0 to 31
- pno_ranks: int32 [32], P('pair'), may hold values from 60 to 120
- fock_off: float32 [64, 64], replicated, may hold values from -1.8 to 1.8
Outputs:
- residual: float32 [32, 2, 14400], P('pair', None, 'aux')
Inputs may be any that keep to these rules, and one draw needn't show every extreme that they name: `neighbours`: neighbour pairs; a pair may be listed more than once and may list itself. `pno_ranks`: rows of a pair's panel from its rank on are padding.
All inputs are finite; a program needn't handle non-finite values.
Results may differ from a plain program's by a relative error of at most 0.0033.
Values may be sent and summed in bfloat16 or wider, within the bound.
A program may use at most 128 MiB of HBM per device.

v0:
```python
import math

import jax
import jax.numpy as jnp
from jax import lax
from jax.sharding import PartitionSpec as P


def side_by_side(arrays, axis, dim, along):
    widths = [math.prod(a.shape[along:]) for a in arrays]
    both = jnp.concatenate(
        [a.reshape(*a.shape[:along], w) for a, w in zip(arrays, widths)], axis=along
    )
    result = lax.all_gather(both, axis, axis=dim, tiled=True)
    blocks = jnp.split(result, [sum(widths[:k]) for k in range(1, len(widths))], axis=along)
    return tuple(
        (b.reshape(*result.shape[:along], *a.shape[along:]) for a, b in zip(arrays, blocks))
    )


def cut_along(shard, dim, length):
    before, after = (shard.shape[:dim], shard.shape[dim + 1 :])
    return jnp.moveaxis(shard.reshape(*before, length, -1, *after), dim, 0)


def sent_and_summed(shard, axis, dim):
    length = lax.axis_size(axis)
    blocks = lax.all_to_all(cut_along(shard, dim, length), axis, 0, 0, tiled=True)
    return jnp.sum(blocks.astype(jnp.float32), axis=0)


def pair_weights(pair_lmo, neighbours, fock_off, first_pair):
    local_pairs = neighbours.shape[0]
    total_pairs = pair_lmo.shape[0]
    lmo_count = fock_off.shape[0]
    lmo_ids = jnp.arange(lmo_count, dtype=jnp.int32)
    own_lmo = lax.dynamic_slice_in_dim(pair_lmo, first_pair, local_pairs, 0)
    own_table = (own_lmo[:, :, None] == lmo_ids[None, None, :]).astype(jnp.float32)
    lmo_table = (pair_lmo[:, :, None] == lmo_ids[None, None, :]).astype(jnp.float32)
    pair_ids = jnp.arange(total_pairs, dtype=jnp.int32)
    onehot = (neighbours[:, :, None] == pair_ids[None, None, :]).astype(jnp.float32)
    fock_rows = jnp.einsum("psl,lm->psm", own_table, fock_off, precision=lax.Precision.HIGHEST)
    near_table = jnp.einsum("pkn,nsl->pksl", onehot, lmo_table)
    values = jnp.sum(fock_rows[:, None, :, :] * near_table, axis=(2, 3))
    weights = jnp.sum(values[:, :, None] * onehot, axis=1).astype(jnp.bfloat16)
    return (weights, own_table)


def project_pairs(slab, amp_block):
    group_size = slab.shape[0]
    matrices = jnp.transpose(amp_block, (0, 2, 1, 3)).reshape(group_size, amp_block.shape[2], -1)
    return jnp.einsum("nra,nrc->nac", slab, matrices, preferred_element_type=jnp.float32).astype(
        jnp.bfloat16
    )


def accumulate(weights, group_limit, running_sum, arriving):
    slab_rows, amp_rows = arriving
    pair_count = slab_rows.shape[0]
    group_size = math.gcd(pair_count, group_limit)

    def group_turn(turn_index, partial_sum):
        offset = turn_index * group_size
        slab = lax.dynamic_slice_in_dim(slab_rows, offset, group_size, 0)
        amp_block = lax.dynamic_slice_in_dim(amp_rows, offset, group_size, 0)
        projected = project_pairs(slab, amp_block)
        coeff_block = lax.dynamic_slice_in_dim(weights, offset, group_size, 1)
        return partial_sum + jnp.einsum(
            "pn,nac->pac", coeff_block, projected, preferred_element_type=jnp.float32
        )

    return lax.fori_loop(0, pair_count // group_size, group_turn, running_sum)


def close_coupling(masked, collected_sum, freq_count):
    local_pairs, rank_dim, aux_width = masked.shape
    collected = collected_sum.astype(jnp.bfloat16)
    coupled = jnp.einsum("pra,pac->prc", masked, collected, preferred_element_type=jnp.float32)
    coupled = jnp.transpose(
        coupled.reshape(local_pairs, rank_dim, freq_count, rank_dim), (0, 2, 1, 3)
    )
    return coupled.reshape(local_pairs, freq_count, rank_dim * rank_dim)


def body(
    panels,
    amplitudes,
    drive,
    pno_energy,
    occ_energy,
    frequency,
    pair_lmo,
    neighbours,
    pno_ranks,
    fock_off,
):
    local_pairs, rank_dim, aux_width = panels.shape
    first_pair = lax.axis_index("pair") * local_pairs
    rows_index = jnp.arange(rank_dim, dtype=jnp.int32)
    keep_rows = rows_index[None, :] < pno_ranks[:, None]
    masked = jnp.where(keep_rows[:, :, None], panels, jnp.zeros_like(panels))
    weights, own_table = pair_weights(pair_lmo, neighbours, fock_off, first_pair)
    start_sum = jnp.zeros((local_pairs, aux_width, 2 * rank_dim), jnp.float32)
    collected_sum = accumulate(
        weights, 4, start_sum, side_by_side((masked, amplitudes), "pair", 0, 1)
    )
    coupled_terms = close_coupling(masked, collected_sum, 2)
    coupled_share = sent_and_summed(coupled_terms.astype(jnp.bfloat16), "aux", 2)
    share_width = drive.shape[2]
    share_start = lax.axis_index("aux") * share_width
    occ_pair = jnp.sum(own_table * occ_energy[None, None, :], axis=(1, 2))
    shift = pno_energy[:, :, None] + pno_energy[:, None, :] - occ_pair[:, None, None]
    shift_flat = lax.dynamic_slice_in_dim(
        shift.reshape(local_pairs, rank_dim * rank_dim), share_start, share_width, 1
    )
    signs = jnp.array([1.0, -1.0], jnp.float32)
    factor = shift_flat[:, None, :] - signs[None, :, None] * frequency[0]
    amp_flat = amplitudes.reshape(local_pairs, 2, rank_dim * rank_dim)
    amp_share = lax.dynamic_slice_in_dim(amp_flat, share_start, share_width, 2).astype(jnp.float32)
    return drive + factor * amp_share + coupled_share


def solution(mesh):
    placed = (
        P("pair", None, "aux"),
        P("pair", None, None, None),
        P("pair", None, "aux"),
        P("pair", None),
        P(),
        P(),
        P(),
        P("pair", None),
        P("pair"),
        P(),
    )
    return jax.shard_map(
        body, mesh=mesh, in_specs=placed, out_specs=P("pair", None, "aux"), check_vma=False
    )
```

profile of v0, /device:TPU:1, one launch (start us, length us, event | category | flops | bytes accessed | tf_op | source)
XLA Modules:
  0.0 392.6 jit_solution(17646866422131770127)
XLA Ops:
  10.8 7.9 %maximum_bitcast_fusion = bf16[1,2,305280]{2,1,0:T(2,128)(2,1)} fusion(bf16[2,28800]{1,0:T(2,128)(2,1)S(1)} %reshape.67, bf16[2,276480]{1,0:T(2,128)(2,1)S(1)} %bitcast.46), kind=kLoop, calls=%fused_computation.10 | loop fusion | flops 2442240 | bytes 2442240
  20.8 214.8 %all-gather.3.cloned.1.call-done = bf16[16,2,305280]{2,1,0:T(2,128)(2,1)} async-done(((bf16[1,2,305280]{2,1,0:T(2,128)(2,1)}), bf16[16,2,305280]{2,1,0:T(2,128)(2,1)}) %all-gather.3.cloned.1.call-update) | async-done | bytes 19537936 | tf_op jit(solution)/shard_map/all_gather | solution.py:14
  235.6 25.7 %reshape.71 = bf16[32,305280]{1,0:T(8,128)(2,1)} reshape(bf16[16,2,305280]{2,1,0:T(2,128)(2,1)} %all-gather.3.cloned.1.call-done) | data formatting | bytes 39075840
  261.3 6.1 %slice-done.1 = bf16[32,276480]{1,0:T(8,128)(2,1)S(1)} async-done(((bf16[32,305280]{1,0:T(8,128)(2,1)}), bf16[32,276480]{1,0:T(8,128)(2,1)S(1)}, s32[]{:S(2)}) %slice-start.1) | async-done | bytes 17694744 | tf_op jit(solution)/shard_map/split | solution.py:15
  267.4 9.7 %copy.33 = bf16[4,8,120,2304]{3,2,1,0:T(8,128)(2,1)} copy(bf16[4,8,120,2304]{3,1,2,0:T(8,128)(2,1)S(1)} %bitcast.43) | data formatting | bytes 35389440
  277.1 5.3 %reshape.69 = bf16[32,2,120,120]{3,2,1,0:T(8,128)(2,1)} reshape(bf16[32,28800]{1,0:T(8,128)(2,1)S(1)} %slice-done) | data formatting | bytes 3686400 | tf_op jit(solution)/shard_map/reshape | solution.py:17
  282.4 81.7 %while.14 = (s32[]{:T(128)}, f32[2,2304,240]{1,0,2:T(2,128)}, bf16[2,32]{1,0:T(2,128)(2,1)S(1)}, bf16[32,120,2304]{2,1,0:T(8,128)(2,1)}, bf16[32,2,120,120]{3,2,...) while((s32[]{:T(128)}, f32[2,2304,240]{1,0,2:T(2,128)}, ...), condition=%wide.region_4.5_spmd.clone, body=%wide.region_3.4_spmd.clone.sunk | while | flops 544112640 | bytes 21058856 | solution.py:72
  283.5 2.9 convolution_convert_fusion.2
  286.5 4.8 %convolution_add_fusion.2 = f32[2,2304,240]{1,0,2:T(2,128)} fusion(f32[2,2304,240]{1,0,2:T(2,128)} %get-tuple-element.179, bf16[4,2304,240]{1,2,0:T(8,128)(2,1)S(1)} %convolution_convert_fusion.2, pred[]{:T(512)S(6)} %compare.3, bf16[2,32]{1,0:T(2,128)(2,1)S(1)} %get-tuple-element.189, s32[]{:T(128)S(6)} %select_n.29), kind=kOutput, calls=%fused_computation.1.clone.1 | convolution fusion | flops 11059200 | bytes 13271173 | tf_op jit(solution)/shard_map/while/body/eval_jaxpr/pn,nac->pac/dot_general | solution.py:68
  292.4 2.9 convolution_convert_fusion.2
  295.3 6.3 %convolution_add_fusion.2 = f32[2,2304,240]{1,0,2:T(2,128)} fusion(f32[2,2304,240]{1,0,2:T(2,128)} %get-tuple-element.179, bf16[4,2304,240]{1,2,0:T(8,128)(2,1)S(1)} %convolution_convert_fusion.2, pred[]{:T(512)S(6)} %compare.3, bf16[2,32]{1,0:T(2,128)(2,1)S(1)} %get-tuple-element.189, s32[]{:T(128)S(6)} %select_n.29), kind=kOutput, calls=%fused_computation.1.clone.1 | convolution fusion | flops 11059200 | bytes 13271173 | tf_op jit(solution)/shard_map/while/body/eval_jaxpr/pn,nac->pac/dot_general | solution.py:68
  302.8 2.9 convolution_convert_fusion.2
  305.7 6.3 %convolution_add_fusion.2 = f32[2,2304,240]{1,0,2:T(2,128)} fusion(f32[2,2304,240]{1,0,2:T(2,128)} %get-tuple-element.179, bf16[4,2304,240]{1,2,0:T(8,128)(2,1)S(1)} %convolution_convert_fusion.2, pred[]{:T(512)S(6)} %compare.3, bf16[2,32]{1,0:T(2,128)(2,1)S(1)} %get-tuple-element.189, s32[]{:T(128)S(6)} %select_n.29), kind=kOutput, calls=%fused_computation.1.clone.1 | convolution fusion | flops 11059200 | bytes 13271173 | tf_op jit(solution)/shard_map/while/body/eval_jaxpr/pn,nac->pac/dot_general | solution.py:68
  316.1 6.3 %convolution_add_fusion.2 = f32[2,2304,240]{1,0,2:T(2,128)} fusion(f32[2,2304,240]{1,0,2:T(2,128)} %get-tuple-element.179, bf16[4,2304,240]{1,2,0:T(8,128)(2,1)S(1)} %convolution_convert_fusion.2, pred[]{:T(512)S(6)} %compare.3, bf16[2,32]{1,0:T(2,128)(2,1)S(1)} %get-tuple-element.189, s32[]{:T(128)S(6)} %select_n.29), kind=kOutput, calls=%fused_computation.1.clone.1 | convolution fusion | flops 11059200 | bytes 13271173 | tf_op jit(solution)/shard_map/while/body/eval_jaxpr/pn,nac->pac/dot_general | solution.py:68
  326.5 6.3 %convolution_add_fusion.2 = f32[2,2304,240]{1,0,2:T(2,128)} fusion(f32[2,2304,240]{1,0,2:T(2,128)} %get-tuple-element.179, bf16[4,2304,240]{1,2,0:T(8,128)(2,1)S(1)} %convolution_convert_fusion.2, pred[]{:T(512)S(6)} %compare.3, bf16[2,32]{1,0:T(2,128)(2,1)S(1)} %get-tuple-element.189, s32[]{:T(128)S(6)} %select_n.29), kind=kOutput, calls=%fused_computation.1.clone.1 | convolution fusion | flops 11059200 | bytes 13271173 | tf_op jit(solution)/shard_map/while/body/eval_jaxpr/pn,nac->pac/dot_general | solution.py:68
  334.0 2.9 convolution_convert_fusion.2
  336.9 6.3 %convolution_add_fusion.2 = f32[2,2304,240]{1,0,2:T(2,128)} fusion(f32[2,2304,240]{1,0,2:T(2,128)} %get-tuple-element.179, bf16[4,2304,240]{1,2,0:T(8,128)(2,1)S(1)} %convolution_convert_fusion.2, pred[]{:T(512)S(6)} %compare.3, bf16[2,32]{1,0:T(2,128)(2,1)S(1)} %get-tuple-element.189, s32[]{:T(128)S(6)} %select_n.29), kind=kOutput, calls=%fused_computation.1.clone.1 | convolution fusion | flops 11059200 | bytes 13271173 | tf_op jit(solution)/shard_map/while/body/eval_jaxpr/pn,nac->pac/dot_general | solution.py:68
  344.4 2.9 convolution_convert_fusion.2
  347.3 6.3 %convolution_add_fusion.2 = f32[2,2304,240]{1,0,2:T(2,128)} fusion(f32[2,2304,240]{1,0,2:T(2,128)} %get-tuple-element.179, bf16[4,2304,240]{1,2,0:T(8,128)(2,1)S(1)} %convolution_convert_fusion.2, pred[]{:T(512)S(6)} %compare.3, bf16[2,32]{1,0:T(2,128)(2,1)S(1)} %get-tuple-element.189, s32[]{:T(128)S(6)} %select_n.29), kind=kOutput, calls=%fused_computation.1.clone.1 | convolution fusion | flops 11059200 | bytes 13271173 | tf_op jit(solution)/shard_map/while/body/eval_jaxpr/pn,nac->pac/dot_general | solution.py:68
  354.8 2.9 convolution_convert_fusion.2
  357.7 6.3 %convolution_add_fusion.2 = f32[2,2304,240]{1,0,2:T(2,128)} fusion(f32[2,2304,240]{1,0,2:T(2,128)} %get-tuple-element.179, bf16[4,2304,240]{1,2,0:T(8,128)(2,1)S(1)} %convolution_convert_fusion.2, pred[]{:T(512)S(6)} %compare.3, bf16[2,32]{1,0:T(2,128)(2,1)S(1)} %get-tuple-element.189, s32[]{:T(128)S(6)} %select_n.29), kind=kOutput, calls=%fused_computation.1.clone.1 | convolution fusion | flops 11059200 | bytes 13271173 | tf_op jit(solution)/shard_map/while/body/eval_jaxpr/pn,nac->pac/dot_general | solution.py:68
  364.1 3.9 convert_element_type.37
  370.0 7.3 %all-to-all-start = ((bf16[16,2,2,900]{3,2,1,0:T(2,128)(2,1)}), bf16[16,2,2,900]{3,2,1,0:T(2,128)(2,1)S(1)}, u32[]{:S(2)}, u32[]{:S(2)}) async-start(bf16[16,2,2,900]{3,2,1,0:T(2,128)(2,1)} %copy.29), calls=%async_computation | async-start | bytes 262144 | tf_op jit(solution)/shard_map/all_to_all | solution.py:28
  377.7 7.2 %all-to-all-done = bf16[16,2,2,900]{3,2,1,0:T(2,128)(2,1)S(1)} async-done(((bf16[16,2,2,900]{3,2,1,0:T(2,128)(2,1)}), bf16[16,2,2,900]{3,2,1,0:T(2,128)(2,1)S(1)}, u32[]{:S(2)}, u32[]{:S(2)}) %all-to-all-start) | async-done | bytes 115232 | tf_op jit(solution)/shard_map/all_to_all | solution.py:28
  (66 shorter events, 23.6 us)
Async XLA Ops:
  6.5 13.6 %copy-start = (f32[64,64]{1,0:T(8,128)S(1)}, f32[64,64]{1,0:T(8,128)}, u32[]{:S(2)}) copy-start(f32[64,64]{1,0:T(8,128)} %param.22) | copy-start | bytes 49156
  6.5 229.0 %all-gather.3.cloned.1.call-start = ((), (), s32[]{:S(2)}) async-start(), calls=%async_computation.1 | async-start | bytes 20759040 | tf_op jit(solution)/shard_map/all_gather | solution.py:14
  10.8 8.7 %copy-start.6 = (s32[32,2]{0,1:T(2,128)S(1)}, s32[32,2]{0,1:T(2,128)}, u32[]{:S(2)}) copy-start(s32[32,2]{0,1:T(2,128)} %param.19) | copy-start | bytes 772
  10.8 8.8 %copy-start.5 = (f32[2,120]{1,0:T(2,128)S(1)}, f32[2,120]{1,0:T(2,128)}, u32[]{:S(2)}) copy-start(f32[2,120]{1,0:T(2,128)} %param.16) | copy-start | bytes 2884
  10.8 9.1 %copy-start.8 = (f32[64]{0:T(128)S(1)}, f32[64]{0:T(128)}, u32[]{:S(2)}) copy-start(f32[64]{0:T(128)} %param.17) | copy-start | bytes 772
  10.8 9.5 %copy-start.7 = (s32[2,8]{1,0:T(2,128)S(1)}, s32[2,8]{1,0:T(2,128)}, u32[]{:S(2)}) copy-start(s32[2,8]{1,0:T(2,128)} %param.20) | copy-start | bytes 196
  261.3 6.1 %slice-start.1 = ((bf16[32,305280]{1,0:T(8,128)(2,1)}), bf16[32,276480]{1,0:T(8,128)(2,1)S(1)}, s32[]{:S(2)}) async-start(bf16[32,305280]{1,0:T(8,128)(2,1)} %reshape.71), calls=%async_computation.3 | async-start | bytes 35389440 | tf_op jit(solution)/shard_map/split | solution.py:15
  267.4 9.7 %slice-start = ((bf16[32,305280]{1,0:T(8,128)(2,1)}), bf16[32,28800]{1,0:T(8,128)(2,1)S(1)}, s32[]{:S(2)}) async-start(bf16[32,305280]{1,0:T(8,128)(2,1)} %reshape.71), calls=%async_computation.2 | async-start | bytes 3686400 | tf_op jit(solution)/shard_map/split | solution.py:15
  364.1 3.9 copy-start.2
  364.1 21.6 %copy-start.1 = (f32[64,64]{1,0:T(8,128)S(1)}, f32[64,64]{1,0:T(8,128)}, u32[]{:S(2)}) copy-start(f32[64,64]{1,0:T(8,128)} %param.22) | copy-start | bytes 49156
  368.0 9.3 %copy-start.9 = (f32[2]{0:T(128)S(1)}, f32[2]{0:T(128)}, u32[]{:S(2)}) copy-start(f32[2]{0:T(128)} %constant.54.clone) | copy-start | bytes 28
  368.0 9.3 %copy-start.3 = (bf16[2,2,120,120]{3,2,1,0:T(8,128)(2,1)S(1)}, bf16[2,2,120,120]{3,2,1,0:T(8,128)(2,1)}, u32[]{:S(2)}) copy-start(bf16[2,2,120,120]{3,2,1,0:T(8,128)(2,1)} %param.14) | copy-start | bytes 345604
  368.0 17.0 %copy-start.4 = (f32[2,2,900]{2,1,0:T(2,128)S(1)}, f32[2,2,900]{2,1,0:T(2,128)}, u32[]{:S(2)}) copy-start(f32[2,2,900]{2,1,0:T(2,128)} %param.15) | copy-start | bytes 43204
  370.0 14.9 %all-to-all-start = ((bf16[16,2,2,900]{3,2,1,0:T(2,128)(2,1)}), bf16[16,2,2,900]{3,2,1,0:T(2,128)(2,1)S(1)}, u32[]{:S(2)}, u32[]{:S(2)}) async-start(bf16[16,2,2,900]{3,2,1,0:T(2,128)(2,1)} %copy.29), calls=%async_computation | async-start | bytes 262144 | tf_op jit(solution)/shard_map/all_to_all | solution.py:28
Sparse Core Ops, SparseCore 0:
  18.9 216.6 all-gather.2
where the time goes:
time: 394 us; the launch traced here: 393 us
  waiting for transfers between devices  222 us (56%)
  matrix products  74 us (19%)
  local copies, waits for them, and re-layouts  59.8 us (15%)
  other arithmetic  15.1 us (4%)
  between operations  14.2 us (4%)
  starting transfers between devices  7.26 us (2%)
    all_gather x1, waiting for transfers between devices, side_by_side(): result = lax.all_gather(both, axis, axis=dim, tiled=True)  215 us
    dot_general x8, matrix products, group_turn(): jnp.einsum('pn,nac->pac', coeff_block, projected, preferred_element_type=...  49.2 us
    unnamed x23, local copies, waits for them, and re-layouts  36.3 us
    dot_general x8, matrix products, project_pairs(): jnp.einsum('nra,nrc->nac', slab, matrices, preferred_element_type=jnp.flo...  23.3 us
    unnamed x3, other arithmetic  9.3 us
    dynamic_slice x16, local copies, waits for them, and re-layouts, group_turn(): amp_block = lax.dynamic_slice_in_dim(amp_rows, offset, group_size, 0)  9.01 us
  transfers between devices with their start and end apart: 2, of which 2 were waited for; matrix products, arithmetic and copies ran while one was open for 0% of the time, Pallas kernels for 0%

commit v1 on v0

--- a/solution.py
+++ b/solution.py
@@ -4,18 +4,6 @@
 import jax.numpy as jnp
 from jax import lax
 from jax.sharding import PartitionSpec as P
-
-
-def side_by_side(arrays, axis, dim, along):
-    widths = [math.prod(a.shape[along:]) for a in arrays]
-    both = jnp.concatenate(
-        [a.reshape(*a.shape[:along], w) for a, w in zip(arrays, widths)], axis=along
-    )
-    result = lax.all_gather(both, axis, axis=dim, tiled=True)
-    blocks = jnp.split(result, [sum(widths[:k]) for k in range(1, len(widths))], axis=along)
-    return tuple(
-        (b.reshape(*result.shape[:along], *a.shape[along:]) for a, b in zip(arrays, blocks))
-    )
 
 
 def cut_along(shard, dim, length):
@@ -46,40 +34,12 @@
     return (weights, own_table)
 
 
-def project_pairs(slab, amp_block):
-    group_size = slab.shape[0]
-    matrices = jnp.transpose(amp_block, (0, 2, 1, 3)).reshape(group_size, amp_block.shape[2], -1)
-    return jnp.einsum("nra,nrc->nac", slab, matrices, preferred_element_type=jnp.float32).astype(
-        jnp.bfloat16
-    )
-
-
-def accumulate(weights, group_limit, running_sum, arriving):
-    slab_rows, amp_rows = arriving
-    pair_count = slab_rows.shape[0]
-    group_size = math.gcd(pair_count, group_limit)
-
-    def group_turn(turn_index, partial_sum):
-        offset = turn_index * group_size
-        slab = lax.dynamic_slice_in_dim(slab_rows, offset, group_size, 0)
-        amp_block = lax.dynamic_slice_in_dim(amp_rows, offset, group_size, 0)
-        projected = project_pairs(slab, amp_block)
-        coeff_block = lax.dynamic_slice_in_dim(weights, offset, group_size, 1)
-        return partial_sum + jnp.einsum(
-            "pn,nac->pac", coeff_block, projected, preferred_element_type=jnp.float32
-        )
-
-    return lax.fori_loop(0, pair_count // group_size, group_turn, running_sum)
-
-
-def close_coupling(masked, collected_sum, freq_count):
+def spread_panels(masked):
     local_pairs, rank_dim, aux_width = masked.shape
-    collected = collected_sum.astype(jnp.bfloat16)
-    coupled = jnp.einsum("pra,pac->prc", masked, collected, preferred_element_type=jnp.float32)
-    coupled = jnp.transpose(
-        coupled.reshape(local_pairs, rank_dim, freq_count, rank_dim), (0, 2, 1, 3)
-    )
-    return coupled.reshape(local_pairs, freq_count, rank_dim * rank_dim)
+    length = lax.axis_size("pair")
+    blocks = cut_along(masked, 2, length)
+    swapped = lax.all_to_all(blocks, "pair", 0, 0, tiled=True)
+    return swapped.reshape(length * local_pairs, rank_dim, aux_width // length)
 
 
 def body(
@@ -100,12 +60,21 @@
     keep_rows = rows_index[None, :] < pno_ranks[:, None]
     masked = jnp.where(keep_rows[:, :, None], panels, jnp.zeros_like(panels))
     weights, own_table = pair_weights(pair_lmo, neighbours, fock_off, first_pair)
-    start_sum = jnp.zeros((local_pairs, aux_width, 2 * rank_dim), jnp.float32)
-    collected_sum = accumulate(
-        weights, 4, start_sum, side_by_side((masked, amplitudes), "pair", 0, 1)
-    )
-    coupled_terms = close_coupling(masked, collected_sum, 2)
-    coupled_share = sent_and_summed(coupled_terms.astype(jnp.bfloat16), "aux", 2)
+    all_weights = lax.all_gather(weights, "pair", axis=0, tiled=True)
+    all_amps = lax.all_gather(amplitudes, "pair", axis=0, tiled=True)
+    slices = spread_panels(masked)
+    projected = jnp.einsum(
+        "naq,nsac->nsqc", slices, all_amps, preferred_element_type=jnp.float32
+    ).astype(jnp.bfloat16)
+    collected = jnp.einsum(
+        "pn,nsqc->psqc", all_weights, projected, preferred_element_type=jnp.float32
+    ).astype(jnp.bfloat16)
+    coupled = jnp.einsum(
+        "paq,psqc->psac", slices, collected, preferred_element_type=jnp.float32
+    ).astype(jnp.bfloat16)
+    coupled = coupled.reshape(coupled.shape[0], 2, rank_dim * rank_dim)
+    over_aux = sent_and_summed(coupled, "aux", 2).astype(jnp.bfloat16)
+    coupled_share = sent_and_summed(over_aux, "pair", 0)
     share_width = drive.shape[2]
     share_start = lax.axis_index("aux") * share_width
     occ_pair = jnp.sum(own_table * occ_energy[None, None, :], axis=(1, 2))

time: 394 us -> 167 us (0.42)
  waiting for transfers between devices: 222 us -> 46.9 us
  matrix products: 74 us -> 6.18 us
  blocking collectives: 0 us -> 54.4 us
  local copies, waits for them, and re-layouts: 59.8 us -> 13.3 us
  starting transfers between devices: 7.26 us -> 27.7 us
  other arithmetic: 15.1 us -> 4.18 us
    all_gather x1, waiting for transfers between devices: 215 us -> 12 us  [body(): all_amps = lax.all_gather(amplitudes, 'pair', axis=0, tiled=True)]
    dot_general x17 -> x3, matrix products: 73.5 us -> 5.7 us  [the longest x1 2.39 us: body(): jnp.einsum('paq,psqc->psac', slices, collected, preferred_element_type=jn...]
    all_gather x0 -> x1, blocking collectives: none -> 54.4 us  [body(): all_weights = lax.all_gather(weights, 'pair', axis=0, tiled=True)]
    unnamed x23 -> x19, local copies, waits for them, and re-layouts: 36.3 us -> 1.76 us
    all_to_all x1 -> x2, waiting for transfers between devices: 7.25 us -> 34.2 us  [sent_and_summed(): lax.all_to_all(cut_along(shard, dim, length), axis, 0, 0, tiled=True)]
    all_to_all x1 -> x2, starting transfers between devices: 7.26 us -> 17.7 us  [sent_and_summed(): lax.all_to_all(cut_along(shard, dim, length), axis, 0, 0, tiled=True)]
    all_to_all x0 -> x1, starting transfers between devices: none -> 10 us  [spread_panels(): swapped = lax.all_to_all(blocks, 'pair', 0, 0, tiled=True)]
    unnamed x3 -> x0, other arithmetic: 9.3 us -> none
  transfers between devices with their start and end apart: 2 -> 4, of which waited for: 2 -> 3; matrix products, arithmetic and copies ran while one was open for 0% -> 3% of each run, Pallas kernels for 0% -> 0%
where the time goes in v1:
time: 167 us
  blocking collectives  54.4 us (33%)
  waiting for transfers between devices  46.9 us (28%)
  starting transfers between devices  27.7 us (17%)
  between operations  14.2 us (9%)
  local copies, waits for them, and re-layouts  13.3 us (8%)
  matrix products  6.18 us (4%)
  other arithmetic  4.18 us (3%)
    all_gather x1, blocking collectives, body(): all_weights = lax.all_gather(weights, 'pair', axis=0, tiled=True)  54.4 us
    all_to_all x2, waiting for transfers between devices, sent_and_summed(): lax.all_to_all(cut_along(shard, dim, length), axis, 0, 0, tiled=True)  34.2 us
    all_to_all x2, starting transfers between devices, sent_and_summed(): lax.all_to_all(cut_along(shard, dim, length), axis, 0, 0, tiled=True)  17.7 us
    all_gather x1, waiting for transfers between devices, body(): all_amps = lax.all_gather(amplitudes, 'pair', axis=0, tiled=True)  12 us
    all_to_all x1, starting transfers between devices, spread_panels(): swapped = lax.all_to_all(blocks, 'pair', 0, 0, tiled=True)  10 us
    transpose x2, local copies, waits for them, and re-layouts, cut_along(): return jnp.moveaxis(shard.reshape(*before, length, -1, *after), dim, 0)  4.61 us
    another operation x1, local copies, waits for them, and re-layouts, cut_along(): return jnp.moveaxis(shard.reshape(*before, length, -1, *after), dim, 0)  3.56 us
  transfers between devices with their start and end apart: 4, of which 3 were waited for; matrix products, arithmetic and copies ran while one was open for 3% of the time, Pallas kernels for 0%

profile of v1, /device:TPU:1, one launch (start us, length us, event | category | flops | bytes accessed | tf_op | source)
XLA Modules:
  0.0 166.8 jit_solution(17784605780855243283)
XLA Ops:
  6.5 0.7 all-gather.3.cloned.1.call-update
  7.3 1.7 %copy.49 = bf16[2,120,2304]{1,2,0:T(8,128)(2,1)S(1)} copy(bf16[2,120,2304]{2,1,0:T(8,128)(2,1)} %param.11) | data formatting | bytes 2211840 | tf_op args[0]
  9.2 1.1 copy.50
  10.3 10.0 %all-to-all-start = ((bf16[16,2,120,144]{2,3,1,0:T(8,128)(2,1)}), bf16[16,2,120,144]{2,3,1,0:T(8,128)(2,1)S(1)}, u32[]{:S(2)}, u32[]{:S(2)}) async-start(bf16[16,2,120,144]{2,3,1,0:T(8,128)(2,1)} %copy.50), calls=%async_computation | async-start | bytes 2359296 | tf_op jit(solution)/shard_map/all_to_all | solution.py:41
  20.4 0.1 copy.48
  20.5 0.2 fusion.10
  20.7 0.3 fusion.9
  21.1 54.4 %all-gather = bf16[16,2,32]{2,1,0:T(2,128)(2,1)S(1)} all-gather(bf16[1,2,32]{2,1,0:T(2,128)(2,1)S(1)} %bitcast.48), channel_id=1, replica_groups=mesh['pair'=16,'aux'=16] {'pair'}, dimensions={0}, use_global_device_ids=true | all-gather | bytes 2176 | tf_op jit(solution)/shard_map/all_gather | solution.py:63
  75.5 12.0 %all-gather.3.cloned.1.call-done = bf16[32,2,120,120]{3,2,1,0:T(8,128)(2,1)} async-done(((bf16[2,2,120,120]{3,2,1,0:T(8,128)(2,1)}), bf16[32,2,120,120]{3,2,1,0:T(8,128)(2,1)}) %all-gather.3.cloned.1.call-update) | async-done | bytes 1843216 | tf_op jit(solution)/shard_map/all_gather | solution.py:64
  87.5 2.3 %convert_bitcast_fusion = bf16[32,2,144,120]{3,2,1,0:T(8,128)(2,1)S(1)} fusion(bf16[32,120,144,1]{1,2,3,0:T(8,128)(2,1)S(1)} %bitcast.43, bf16[32,2,120,120]{3,2,1,0:T(8,128)(2,1)} %all-gather.3.cloned.1.call-done), kind=kOutput, calls=%fused_computation.4 | convolution fusion | flops 266526720 | bytes 5160960 | tf_op jit(solution)/shard_map/naq,nsac->nsqc/dot_general | solution.py:66
  89.8 1.0 fusion.4
  90.8 2.4 %convert_bitcast_fusion.1 = bf16[32,2,120,120]{2,3,1,0:T(8,128)(2,1)S(1)} fusion(bf16[32,120,144,1]{1,2,3,0:T(8,128)(2,1)S(1)} %bitcast.44, bf16[32,2,144,120]{3,0,2,1:T(8,128)(2,1)S(1)} %fusion.4), kind=kOutput, calls=%fused_computation.6 | convolution fusion | flops 266342400 | bytes 5160960 | tf_op jit(solution)/shard_map/paq,psqc->psac/dot_general | solution.py:72
  93.2 2.6 %copy.53 = bf16[32,2,120,120]{3,2,1,0:T(8,128)(2,1)} copy(bf16[32,2,120,120]{2,3,1,0:T(8,128)(2,1)S(1)} %convert_bitcast_fusion.1) | data formatting | bytes 3686400 | tf_op jit(solution)/shard_map/convert_element_type | solution.py:74
  95.8 3.6 %reshape_reshape.3 = bf16[32,2,16,900]{3,2,1,0:T(8,128)(2,1)S(1)} reshape(bf16[32,2,120,120]{3,2,1,0:T(8,128)(2,1)} %copy.53) | data formatting | bytes 3686400 | tf_op jit(solution)/shard_map/reshape;reshape | solution.py:11
  99.4 3.5 %copy.54 = bf16[16,32,2,900]{3,2,1,0:T(2,128)(2,1)} copy(bf16[16,32,2,900]{3,0,2,1:T(8,128)(2,1)S(1)} %bitcast.45) | data formatting | bytes 3686400 | tf_op jit(solution)/shard_map/transpose | solution.py:11
  102.9 14.2 %all-to-all-start.1 = ((bf16[16,32,2,900]{3,2,1,0:T(2,128)(2,1)}), bf16[16,32,2,900]{3,2,1,0:T(2,128)(2,1)S(1)}, u32[]{:S(2)}, u32[]{:S(2)}) async-start(bf16[16,32,2,900]{3,2,1,0:T(2,128)(2,1)} %copy.54), calls=%async_computation.1 | async-start | bytes 4194304 | tf_op jit(solution)/shard_map/all_to_all | solution.py:16
  117.1 0.3 reshape.49
  117.5 0.2 add.33
  118.4 0.2 select_reduce_fusion.1
  118.6 26.7 %all-to-all-done.1 = bf16[16,32,2,900]{3,2,1,0:T(2,128)(2,1)S(1)} async-done(((bf16[16,32,2,900]{3,2,1,0:T(2,128)(2,1)}), bf16[16,32,2,900]{3,2,1,0:T(2,128)(2,1)S(1)}, u32[]{:S(2)}, u32[]{:S(2)}) %all-to-all-start.1) | async-done | bytes 1843232 | tf_op jit(solution)/shard_map/all_to_all | solution.py:16
  145.4 2.8 %reduce_sum.51 = bf16[32,2,900]{2,1,0:T(2,128)(2,1)} reduce(bf16[16,32,2,900]{3,2,1,0:T(2,128)(2,1)S(1)} %all-to-all-done.1, bf16[]{:T(256)} %constant.25.clone.1), dimensions={0}, to_apply=%region_3.4 | reduce | flops 864000 | bytes 1958402 | tf_op jit(solution)/shard_map/reduce_sum | solution.py:17
  148.2 3.5 %all-to-all-start.2 = ((bf16[16,2,2,900]{3,2,1,0:T(2,128)(2,1)}), bf16[16,2,2,900]{3,2,1,0:T(2,128)(2,1)S(1)}, u32[]{:S(2)}, u32[]{:S(2)}) async-start(bf16[16,2,2,900]{3,2,1,0:T(2,128)(2,1)} %bitcast.17), calls=%async_computation.2 | async-start | bytes 262144 | tf_op jit(solution)/shard_map/all_to_all | solution.py:16
  151.7 7.4 %all-to-all-done.2 = bf16[16,2,2,900]{3,2,1,0:T(2,128)(2,1)S(1)} async-done(((bf16[16,2,2,900]{3,2,1,0:T(2,128)(2,1)}), bf16[16,2,2,900]{3,2,1,0:T(2,128)(2,1)S(1)}, u32[]{:S(2)}, u32[]{:S(2)}) %all-to-all-start.2) | async-done | bytes 115232 | tf_op jit(solution)/shard_map/all_to_all | solution.py:16
  159.3 0.7 add_add_fusion
  (28 shorter events, 0.6 us)
Async XLA Ops:
  6.5 14.0 %copy-start = (f32[64,64]{1,0:T(8,128)S(1)}, f32[64,64]{1,0:T(8,128)}, u32[]{:S(2)}) copy-start(f32[64,64]{1,0:T(8,128)} %param.20) | copy-start | bytes 49156
  6.5 2.5 %copy-start.7 = (s32[2]{0:T(128)S(1)}, s32[2]{0:T(128)}, u32[]{:S(2)}) copy-start(s32[2]{0:T(128)} %param.19) | copy-start | bytes 28
  6.5 80.9 %all-gather.3.cloned.1.call-start = ((), (), s32[]{:S(2)}) async-start(), calls=%async_computation.3 | async-start | bytes 2088960 | tf_op jit(solution)/shard_map/all_gather | solution.py:64
  9.2 11.2 %copy-start.4 = (s32[32,2]{0,1:T(2,128)S(1)}, s32[32,2]{0,1:T(2,128)}, u32[]{:S(2)}) copy-start(s32[32,2]{0,1:T(2,128)} %param.17) | copy-start | bytes 772
  9.2 11.6 %copy-start.5 = (s32[2,8]{1,0:T(2,128)S(1)}, s32[2,8]{1,0:T(2,128)}, u32[]{:S(2)}) copy-start(s32[2,8]{1,0:T(2,128)} %param.18) | copy-start | bytes 196
  10.3 65.2 %all-to-all-start = ((bf16[16,2,120,144]{2,3,1,0:T(8,128)(2,1)}), bf16[16,2,120,144]{2,3,1,0:T(8,128)(2,1)S(1)}, u32[]{:S(2)}, u32[]{:S(2)}) async-start(bf16[16,2,120,144]{2,3,1,0:T(8,128)(2,1)} %copy.50), calls=%async_computation | async-start | bytes 2359296 | tf_op jit(solution)/shard_map/all_to_all | solution.py:41
  102.9 14.2 %copy-start.1 = (bf16[2,2,120,120]{3,2,1,0:T(8,128)(2,1)S(1)}, bf16[2,2,120,120]{3,2,1,0:T(8,128)(2,1)}, u32[]{:S(2)}) copy-start(bf16[2,2,120,120]{3,2,1,0:T(8,128)(2,1)} %param.12) | copy-start | bytes 345604
  102.9 14.5 %copy-start.3 = (f32[2,120]{1,0:T(2,128)S(1)}, f32[2,120]{1,0:T(2,128)}, u32[]{:S(2)}) copy-start(f32[2,120]{1,0:T(2,128)} %param.14) | copy-start | bytes 2884
  102.9 15.5 %copy-start.6 = (f32[64]{0:T(128)S(1)}, f32[64]{0:T(128)}, u32[]{:S(2)}) copy-start(f32[64]{0:T(128)} %param.15) | copy-start | bytes 772
  102.9 42.5 %all-to-all-start.1 = ((bf16[16,32,2,900]{3,2,1,0:T(2,128)(2,1)}), bf16[16,32,2,900]{3,2,1,0:T(2,128)(2,1)S(1)}, u32[]{:S(2)}, u32[]{:S(2)}) async-start(bf16[16,32,2,900]{3,2,1,0:T(2,128)(2,1)} %copy.54), calls=%async_computation.1 | async-start | bytes 4194304 | tf_op jit(solution)/shard_map/all_to_all | solution.py:16
  117.0 34.7 %copy-start.8 = (f32[2]{0:T(128)S(1)}, f32[2]{0:T(128)}, u32[]{:S(2)}) copy-start(f32[2]{0:T(128)} %constant.26.clone) | copy-start | bytes 28
  117.1 42.2 %copy-start.2 = (f32[2,2,900]{2,1,0:T(2,128)S(1)}, f32[2,2,900]{2,1,0:T(2,128)}, u32[]{:S(2)}) copy-start(f32[2,2,900]{2,1,0:T(2,128)} %param.13) | copy-start | bytes 43204
  148.2 11.0 %all-to-all-start.2 = ((bf16[16,2,2,900]{3,2,1,0:T(2,128)(2,1)}), bf16[16,2,2,900]{3,2,1,0:T(2,128)(2,1)S(1)}, u32[]{:S(2)}, u32[]{:S(2)}) async-start(bf16[16,2,2,900]{3,2,1,0:T(2,128)(2,1)} %bitcast.17), calls=%async_computation.2 | async-start | bytes 262144 | tf_op jit(solution)/shard_map/all_to_all | solution.py:16
Sparse Core Ops, SparseCore 0:
  9.1 78.2 all-gather.2

commit v2 on v1

v2 whole, which is shorter than its diff:
```python
import jax
import jax.numpy as jnp
from jax import lax
from jax.experimental import pallas as pl
from jax.experimental.pallas import tpu as pltpu
from jax.sharding import PartitionSpec as P

MESH = pl.DeviceIdType.MESH

PAIR_STEPS = [(1, 0)] + [(dx, dz) for dz in (1, 7, 2, 6, 3, 5, 4) for dx in (0, 1)]
CHIP_STEPS = [(0, 1), (1, 0), (3, 0), (1, 1), (3, 1), (2, 0), (2, 1)]
GROUP = 4


def kernel(
    mt_ref,
    amp_ref,
    nbr_ref,
    wgt_ref,
    out_ref,
    mbuf,
    abuf,
    nbuf,
    wbuf,
    nsm,
    wsm,
    proj,
    mtr,
    coll,
    sbuf,
    rbuf,
    tbuf,
    ubuf,
    fin,
    m_send,
    m_recv,
    f_send,
    f_recv,
    a_send,
    a_recv,
    g_send,
    g_recv,
    c_send,
    c_recv,
    n_send,
    n_recv,
    w_send,
    w_recv,
    s_sem,
    r_send,
    r_recv,
    u_send,
    u_recv,
    x_send,
    x_recv,
):
    pair = lax.axis_index("pair")
    aux = lax.axis_index("aux")
    xlo, z = pair // 8, lax.rem(pair, 8)
    chip, core = aux // 2, lax.rem(aux, 2)
    y, xhi = chip // 2, lax.rem(chip, 2)
    other = 1 - core
    partner = (pair, chip * 2 + other)

    def pair_to(step):
        dx, dz = step
        return lax.rem(xlo + dx, 2) * 8 + lax.rem(z + dz, 8)

    def pair_from(step):
        dx, dz = step
        return lax.rem(xlo + dx, 2) * 8 + lax.rem(z + 8 - dz, 8)

    def chip_to(step):
        dy, dx = step
        return lax.rem(y + dy, 4) * 2 + lax.rem(xhi + dx, 2)

    def chip_from(step):
        dy, dx = step
        return lax.rem(y + 4 - dy, 4) * 2 + lax.rem(xhi + dx, 2)

    barrier = pltpu.get_barrier_semaphore()
    for step in PAIR_STEPS:
        pl.semaphore_signal(barrier, inc=1, device_id=(pair_from(step), aux), device_id_type=MESH)
    for step in CHIP_STEPS:
        pl.semaphore_signal(
            barrier, inc=1, device_id=(pair, chip_from(step) * 2 + core), device_id_type=MESH
        )
    pl.semaphore_signal(barrier, inc=1, device_id=partner, device_id_type=MESH)

    def remote(src, dst, send, recv, target):
        return pltpu.make_async_remote_copy(
            src_ref=src,
            dst_ref=dst,
            send_sem=send,
            recv_sem=recv,
            device_id=target,
            device_id_type=MESH,
        )

    def m_rows(p):
        return mt_ref.at[:, pl.ds(pl.multiple_of(p * 144, 16), 144), :]

    abuf[chip, core, pair] = amp_ref[...]
    nbuf[pair] = nbr_ref[...]
    wbuf[pair] = wgt_ref[...]
    pl.semaphore_wait(barrier, 23)

    for i, step in enumerate(PAIR_STEPS):
        to = (pair_to(step), aux)
        remote(amp_ref, abuf.at[chip, core, pair], a_send.at[i], a_recv.at[i], to).start()
        remote(nbr_ref, nbuf.at[pair], n_send.at[i], n_recv.at[i], to).start()
        remote(wgt_ref, wbuf.at[pair], w_send.at[i], w_recv.at[i], to).start()
    for i, step in enumerate(PAIR_STEPS):
        p = pair_to(step)
        remote(m_rows(p), mbuf.at[pair, core], m_send.at[i], m_recv.at[i], (p, aux)).start()
    own_to_partner = remote(
        m_rows(pair), mbuf.at[pair, core], f_send.at[15], f_recv.at[15], partner
    )
    own_to_partner.start()
    mbuf[pair, core] = mt_ref[:, pl.ds(pl.multiple_of(pair * 144, 16), 144), :]

    for i, step in enumerate(PAIR_STEPS):
        p = pair_from(step)
        remote(amp_ref, abuf.at[chip, core, p], a_send.at[i], a_recv.at[i], (p, aux)).wait_recv()
    for i, step in enumerate(CHIP_STEPS):
        to = (pair, chip_to(step) * 2 + core)
        remote(
            abuf.at[chip, core], abuf.at[chip, core], g_send.at[i], g_recv.at[i], to
        ).start()
    remote(
        abuf.at[chip, core], abuf.at[chip, core], c_send.at[7], c_recv.at[7], partner
    ).start()

    for i, step in enumerate(PAIR_STEPS):
        p = pair_from(step)
        remote(nbr_ref, nbuf.at[p], n_send.at[i], n_recv.at[i], (p, aux)).wait_recv()
        remote(wgt_ref, wbuf.at[p], w_send.at[i], w_recv.at[i], (p, aux)).wait_recv()
    to_nsm = pltpu.make_async_copy(nbuf, nsm, s_sem.at[0])
    to_wsm = pltpu.make_async_copy(wbuf, wsm, s_sem.at[1])
    to_nsm.start()
    to_wsm.start()
    to_nsm.wait()
    to_wsm.wait()

    def relay_block(i):
        step = PAIR_STEPS[i]
        p = pair_from(step)
        remote(m_rows(p), mbuf.at[p, core], m_send.at[i], m_recv.at[i], (p, aux)).wait_recv()
        remote(
            mbuf.at[p, core], mbuf.at[p, core], f_send.at[i], f_recv.at[i], partner
        ).start()

    def relayed(i):
        p = pair if i == 15 else pair_from(PAIR_STEPS[i])
        remote(
            mbuf.at[p, other], mbuf.at[p, other], f_send.at[i], f_recv.at[i], partner
        ).wait_recv()
        for h in range(2):
            mtr[p, h] = mbuf[p, h, core].T
        return p

    def project(p):
        for c in range(2):
            matrix = abuf[:, c, p].reshape(128, 256)
            for h in range(2):
                proj[2 * p + c, h] = jnp.dot(
                    mbuf[p, h, c], matrix, preferred_element_type=jnp.float32
                ).astype(jnp.bfloat16)

    early = 9
    relayed(15)
    for i in range(early):
        relay_block(i)
        if i:
            relayed(i - 1)
    for i, step in enumerate(CHIP_STEPS):
        g = chip_from(step)
        remote(
            abuf.at[g, core], abuf.at[g, core], g_send.at[i], g_recv.at[i], (pair, g * 2 + core)
        ).wait_recv()
        remote(abuf.at[g, core], abuf.at[g, core], c_send.at[i], c_recv.at[i], partner).start()
    relayed(early - 1)
    relay_block(early)
    for i in range(8):
        g = chip if i == 7 else chip_from(CHIP_STEPS[i])
        remote(
            abuf.at[g, other], abuf.at[g, other], c_send.at[i], c_recv.at[i], partner
        ).wait_recv()
    project(pair)
    for i in range(early):
        project(pair_from(PAIR_STEPS[i]))
    for i in range(early, 15):
        if i + 1 < 15:
            relay_block(i + 1)
        project(relayed(i))

    def one_pair(p):
        for h in range(2):
            total = jnp.zeros((144, 256), jnp.float32)
            for k in range(8):
                n = nsm[p, 0, core * 8 + k]
                w = wsm[p, 0, core * 8 + k]
                total = total + w * proj[n, h].astype(jnp.float32)
            coll[h] = total.astype(jnp.bfloat16)
        closed = jnp.dot(mtr[p, 0], coll[0], preferred_element_type=jnp.float32)
        closed = closed + jnp.dot(mtr[p, 1], coll[1], preferred_element_type=jnp.float32)
        sbuf[:, p] = closed.astype(jnp.bfloat16).reshape(8, 16, 256)

    def part(q):
        return pl.ds(q * GROUP, GROUP)

    groups = 16 // GROUP
    for q in range(groups):
        lax.fori_loop(q * GROUP, (q + 1) * GROUP, lambda p, x: (one_pair(p), x)[1], 0)
        for i, step in enumerate(CHIP_STEPS):
            g = chip_to(step)
            remote(
                sbuf.at[g, part(q)],
                rbuf.at[i, part(q)],
                r_send.at[q, i],
                r_recv.at[q, i],
                (pair, g * 2 + core),
            ).start()
    for q in range(groups):
        for i, step in enumerate(CHIP_STEPS):
            g = chip_from(step)
            remote(
                sbuf.at[g, part(q)],
                rbuf.at[i, part(q)],
                r_send.at[q, i],
                r_recv.at[q, i],
                (pair, g * 2 + core),
            ).wait_recv()
        total = sbuf[chip, part(q)].astype(jnp.float32)
        for i in range(7):
            total = total + rbuf[i, part(q)].astype(jnp.float32)
        tbuf[part(q)] = total.astype(jnp.bfloat16)
        for j in range(GROUP):
            p = q * GROUP + j
            slot = lax.rem(xlo + p // 8, 2) * 8 + lax.rem(p % 8 - z + 8, 8)

            @pl.when(p != pair)
            def _():
                remote(
                    tbuf.at[p], ubuf.at[slot], u_send.at[slot], u_recv.at[slot], (p, aux)
                ).start()

    total = tbuf[pair].astype(jnp.float32)
    for slot in range(1, 16):
        p = pair_from((slot // 8, slot % 8))
        remote(
            tbuf.at[p], ubuf.at[slot], u_send.at[slot], u_recv.at[slot], (p, aux)
        ).wait_recv()
        total = total + ubuf[slot].astype(jnp.float32)
    fin[core] = total
    swap = remote(fin.at[core], fin.at[core], x_send, x_recv, partner)
    swap.start()
    out_ref[core] = total
    remote(fin.at[other], fin.at[other], x_send, x_recv, partner).wait_recv()
    out_ref[other] = fin[other]

    for i, step in enumerate(PAIR_STEPS):
        to = (pair_to(step), aux)
        remote(amp_ref, abuf.at[chip, core, pair], a_send.at[i], a_recv.at[i], to).wait_send()
        remote(nbr_ref, nbuf.at[pair], n_send.at[i], n_recv.at[i], to).wait_send()
        remote(wgt_ref, wbuf.at[pair], w_send.at[i], w_recv.at[i], to).wait_send()
        p = pair_to(step)
        remote(m_rows(p), mbuf.at[pair, core], m_send.at[i], m_recv.at[i], to).wait_send()
        p = pair_from(step)
        remote(
            mbuf.at[p, core], mbuf.at[p, core], f_send.at[i], f_recv.at[i], partner
        ).wait_send()
    own_to_partner.wait_send()
    for i, step in enumerate(CHIP_STEPS):
        to = (pair, chip_to(step) * 2 + core)
        remote(
            abuf.at[chip, core], abuf.at[chip, core], g_send.at[i], g_recv.at[i], to
        ).wait_send()
        for q in range(groups):
            remote(
                sbuf.at[chip, part(q)], rbuf.at[i, part(q)], r_send.at[q, i], r_recv.at[q, i], to
            ).wait_send()
        g = chip_from(step)
        remote(abuf.at[g, core], abuf.at[g, core], c_send.at[i], c_recv.at[i], partner).wait_send()
    remote(
        abuf.at[chip, core], abuf.at[chip, core], c_send.at[7], c_recv.at[7], partner
    ).wait_send()
    for slot in range(1, 16):
        p = pair_to((slot // 8, slot % 8))
        remote(
            tbuf.at[p], ubuf.at[slot], u_send.at[slot], u_recv.at[slot], (p, aux)
        ).wait_send()
    swap.wait_send()


def coupled_rows(mt, amp_piece, nbr_row, wgt_row):
    bf16, f32, i32 = jnp.bfloat16, jnp.float32, jnp.int32
    dma = pltpu.SemaphoreType.DMA
    groups = 16 // GROUP
    return pl.pallas_call(
        kernel,
        out_shape=jax.ShapeDtypeStruct((2, 16, 256), f32),
        in_specs=[pl.BlockSpec(memory_space=pltpu.VMEM)] * 4,
        out_specs=pl.BlockSpec(memory_space=pltpu.VMEM),
        scratch_shapes=[
            pltpu.VMEM((16, 2, 2, 144, 128), bf16),
            pltpu.VMEM((8, 2, 16, 16, 256), bf16),
            pltpu.VMEM((16, 1, 128), i32),
            pltpu.VMEM((16, 1, 128), f32),
            pltpu.SMEM((16, 1, 128), i32),
            pltpu.SMEM((16, 1, 128), f32),
            pltpu.VMEM((32, 2, 144, 256), bf16),
            pltpu.VMEM((16, 2, 128, 144), bf16),
            pltpu.VMEM((2, 144, 256), bf16),
            pltpu.VMEM((8, 16, 16, 256), bf16),
            pltpu.VMEM((7, 16, 16, 256), bf16),
            pltpu.VMEM((16, 16, 256), bf16),
            pltpu.VMEM((16, 16, 256), bf16),
            pltpu.VMEM((2, 16, 256), f32),
            dma((15,)),
            dma((15,)),
            dma((16,)),
            dma((16,)),
            dma((15,)),
            dma((15,)),
            dma((7,)),
            dma((7,)),
            dma((8,)),
            dma((8,)),
            dma((15,)),
            dma((15,)),
            dma((15,)),
            dma((15,)),
            dma((2,)),
            dma((groups, 7)),
            dma((groups, 7)),
            dma((16,)),
            dma((16,)),
            dma,
            dma,
        ],
        compiler_params=pltpu.CompilerParams(
            collective_id=0, has_side_effects=True, vmem_limit_bytes=56 << 20
        ),
        name="coupled_rows",
    )(mt, amp_piece, nbr_row, wgt_row)


def slot_weights(pair_lmo, neighbours, fock_off, first_pair):
    local_pairs, slots = neighbours.shape
    total_pairs = pair_lmo.shape[0]
    lmo_count = fock_off.shape[0]
    lmo_ids = jnp.arange(lmo_count, dtype=jnp.int32)
    own_lmo = lax.dynamic_slice_in_dim(pair_lmo, first_pair, local_pairs, 0)
    own_table = (own_lmo[:, :, None] == lmo_ids[None, None, :]).astype(jnp.float32)
    lmo_table = (pair_lmo[:, :, None] == lmo_ids[None, None, :]).astype(jnp.float32)
    pair_ids = jnp.arange(total_pairs, dtype=jnp.int32)
    onehot = (neighbours[:, :, None] == pair_ids[None, None, :]).astype(jnp.float32)
    fock_rows = jnp.einsum("psl,lm->psm", own_table, fock_off, precision=lax.Precision.HIGHEST)
    near_table = jnp.einsum("pkn,nsl->pksl", onehot, lmo_table)
    values = jnp.sum(fock_rows[:, None, :, :] * near_table, axis=(2, 3))
    same = neighbours[:, :, None] == neighbours[:, None, :]
    summed = jnp.sum(jnp.where(same, values[:, None, :], 0.0), axis=2)
    rounded = summed.astype(jnp.bfloat16).astype(jnp.float32)
    slot_ids = jnp.arange(slots, dtype=jnp.int32)
    earlier = same & (slot_ids[None, None, :] < slot_ids[None, :, None])
    repeated = jnp.any(earlier, axis=2)
    return jnp.where(repeated, 0.0, rounded), own_table


def row_of(values):
    flat = values.reshape(1, -1)
    return jnp.pad(flat, ((0, 0), (0, 128 - flat.shape[1])))


def body(
    panels,
    amplitudes,
    drive,
    pno_energy,
    occ_energy,
    frequency,
    pair_lmo,
    neighbours,
    pno_ranks,
    fock_off,
):
    local_pairs, rank_dim, aux_width = panels.shape
    first_pair = lax.axis_index("pair") * local_pairs
    aux = lax.axis_index("aux")
    chip, core = aux // 2, lax.rem(aux, 2)
    rows_index = jnp.arange(rank_dim, dtype=jnp.int32)
    keep_rows = rows_index[None, :] < pno_ranks[:, None]
    masked = jnp.where(keep_rows[:, :, None], panels, jnp.zeros_like(panels))
    masked = masked.reshape(local_pairs, 8, 15, aux_width)
    masked = jnp.pad(masked, ((0, 0), (0, 0), (0, 1), (0, 0)))
    mt = jnp.transpose(masked.reshape(local_pairs, 128, aux_width), (0, 2, 1))
    weights, own_table = slot_weights(pair_lmo, neighbours, fock_off, first_pair)
    piece = lax.dynamic_slice(
        amplitudes, (core, 0, chip * 15, 0), (1, 2, 15, rank_dim)
    )[0]
    piece = jnp.pad(jnp.transpose(piece, (1, 0, 2)), ((0, 1), (0, 0), (0, 8)))
    rows = coupled_rows(mt, piece.reshape(16, 256), row_of(neighbours), row_of(weights))
    rows = rows.reshape(local_pairs, 16, 2, 128)[:, :15, :, :rank_dim]
    rows = jnp.transpose(rows, (0, 2, 1, 3)).reshape(local_pairs, 2, 15 * rank_dim)
    share_width = drive.shape[2]
    coupled_share = lax.dynamic_slice_in_dim(rows, core * share_width, share_width, 2)
    share_start = aux * share_width
    occ_pair = jnp.sum(own_table * occ_energy[None, None, :], axis=(1, 2))
    shift = pno_energy[:, :, None] + pno_energy[:, None, :] - occ_pair[:, None, None]
    shift_flat = lax.dynamic_slice_in_dim(
        shift.reshape(local_pairs, rank_dim * rank_dim), share_start, share_width, 1
    )
    signs = jnp.array([1.0, -1.0], jnp.float32)
    factor = shift_flat[:, None, :] - signs[None, :, None] * frequency[0]
    amp_flat = amplitudes.reshape(local_pairs, 2, rank_dim * rank_dim)
    amp_share = lax.dynamic_slice_in_dim(amp_flat, share_start, share_width, 2).astype(jnp.float32)
    return drive + factor * amp_share + coupled_share


def solution(mesh):
    placed = (
        P("pair", None, "aux"),
        P("pair", None, None, None),
        P("pair", None, "aux"),
        P("pair", None),
        P(),
        P(),
        P(),
        P("pair", None),
        P("pair"),
        P(),
    )
    return jax.shard_map(
        body, mesh=mesh, in_specs=placed, out_specs=P("pair", None, "aux"), check_vma=False
    )
```

time: 167 us -> 83.6 us (0.50)
  the two profiles are of different devices: /device:TPU:1 before, /device:TPU:3 now
where the time goes in v2:
time: 83.6 us; the launch traced here: 83.4 us
  Pallas kernels  70.4 us (84%)
  local copies, waits for them, and re-layouts  8.07 us (10%)
  other arithmetic  3.56 us (4%)
  between operations  0.85 us (1%)
    pallas_call x1, Pallas kernels, coupled_rows(): pl.pallas_call(kernel, out_shape=jax.ShapeDtypeStruct((2, 16, 256), f32),...  70.4 us
    reshape x1, local copies, waits for them, and re-layouts, body(): mt = jnp.transpose(masked.reshape(local_pairs, 128, aux_width), (0, 2, 1))  2.78 us

profile of v2, /device:TPU:3, one launch (start us, length us, event | category | flops | bytes accessed | tf_op | source)
XLA Modules:
  0.0 83.4 jit_solution(1666893196933492849)
XLA Ops:
  0.0 0.7 iota_compare_fusion.5
  0.7 1.4 %broadcast_select_fusion = bf16[2,120,2304]{2,1,0:T(8,128)(2,1)S(1)} fusion(bf16[2,120,2304]{2,1,0:T(8,128)(2,1)} %param.11, pred[2,120]{1,0:T(4,128)(4,1)S(1)} %iota_compare_fusion.5), kind=kLoop, calls=%fused_computation.2 | loop fusion | flops 552960 | bytes 2212080 | tf_op jit(solution)/shard_map/jit(_where)/select_n | solution.py:394
  2.1 0.9 %copy.22 = bf16[2,120,2304]{2,0,1:T(2,128)(2,1)S(1)} copy(bf16[2,120,2304]{2,1,0:T(8,128)(2,1)S(1)} %broadcast_select_fusion) | data formatting | bytes 2211840 | tf_op jit(solution)/shard_map/jit(_where)/select_n | solution.py:394
  3.0 0.9 %pad.16 = bf16[2,8,16,2304]{3,0,2,1:T(2,128)(2,1)S(1)} pad(bf16[2,8,15,2304]{3,0,2,1:T(2,128)(2,1)S(1)} %bitcast.32, bf16[]{:T(256)} %constant.39.clone.1), padding=0_0x0_0x0_1x0_0 | pad | bytes 2285570 | tf_op jit(solution)/shard_map/jit(_pad)/pad | solution.py:396
  3.9 2.8 %copy.24 = bf16[2,128,2304]{1,2,0:T(8,128)(2,1)} copy(bf16[2,128,2304]{2,0,1:T(2,128)(2,1)S(1)} %bitcast.30) | data formatting | bytes 2359296 | tf_op jit(solution)/shard_map/reshape | solution.py:397
  6.8 0.6 copy.36
  7.4 0.1 reshape.106
  7.5 0.5 pad.18.nbr_ref
  8.0 0.2 fusion.9
  8.3 0.1 copy.21
  8.4 0.2 fusion.1
  8.6 0.3 fusion
  8.9 0.2 fusion.6
  9.1 0.1 select_n.51
  9.2 0.5 pad.19.wgt_ref
  9.7 70.4 %coupled_rows.1 = f32[2,16,256]{2,1,0:T(8,128)} custom-call(bf16[2,2304,128]{2,1,0:T(8,128)(2,1)} %bitcast.31, bf16[16,256]{1,0:T(8,128)(2,1)} %bitcast.34, s32[1,128]{1,0:T(1,128)} %pad.18.nbr_ref, f32[1,128]{1,0:T(1,128)} %pad.19.wgt_ref), custom_call_target="tpu_custom_call" | custom-call | tf_op jit(solution)/shard_map/coupled_rows/pallas_call | solution.py:300
  80.1 0.8 reshape.107
  80.9 0.1 reshape.108
  81.0 0.3 reshape.102
  81.4 0.1 broadcast_add_fusion
  81.5 0.2 add.51
  81.7 0.2 select_reduce_fusion
  81.9 0.1 dynamic-slice_subtract_fusion
  82.6 0.7 dynamic-slice_add_fusion
  (25 shorter events, 0.2 us)
Async XLA Ops:
  0.0 8.4 %copy-start = (f32[64,64]{1,0:T(8,128)S(1)}, f32[64,64]{1,0:T(8,128)}, u32[]{:S(2)}) copy-start(f32[64,64]{1,0:T(8,128)} %param.20) | copy-start | bytes 49156
  3.9 2.8 %copy-start.1 = (bf16[2,2,120,120]{3,2,1,0:T(8,128)(2,1)S(1)}, bf16[2,2,120,120]{3,2,1,0:T(8,128)(2,1)}, u32[]{:S(2)}) copy-start(bf16[2,2,120,120]{3,2,1,0:T(8,128)(2,1)} %param.12) | copy-start | bytes 345604
  3.9 3.5 %copy-start.2 = (s32[2,8]{1,0:T(2,128)S(1)}, s32[2,8]{1,0:T(2,128)}, u32[]{:S(2)}) copy-start(s32[2,8]{1,0:T(2,128)} %param.18) | copy-start | bytes 196
  3.9 4.3 %copy-start.5 = (s32[32,2]{0,1:T(2,128)S(1)}, s32[32,2]{0,1:T(2,128)}, u32[]{:S(2)}) copy-start(s32[32,2]{0,1:T(2,128)} %param.17) | copy-start | bytes 772
  6.7 74.7 %copy-start.4 = (f32[2,120]{1,0:T(2,128)S(1)}, f32[2,120]{1,0:T(2,128)}, u32[]{:S(2)}) copy-start(f32[2,120]{1,0:T(2,128)} %param.14) | copy-start | bytes 2884
  8.6 73.1 %copy-start.6 = (f32[64]{0:T(128)S(1)}, f32[64]{0:T(128)}, u32[]{:S(2)}) copy-start(f32[64]{0:T(128)} %param.15) | copy-start | bytes 772
  8.6 74.0 %copy-start.7 = (f32[2]{0:T(128)S(1)}, f32[2]{0:T(128)}, u32[]{:S(2)}) copy-start(f32[2]{0:T(128)} %constant.46.clone) | copy-start | bytes 28
  8.6 74.0 %copy-start.3 = (f32[2,2,900]{2,1,0:T(2,128)S(1)}, f32[2,2,900]{2,1,0:T(2,128)}, u32[]{:S(2)}) copy-start(f32[2,2,900]{2,1,0:T(2,128)} %param.13) | copy-start | bytes 43204

commit v3 on v1

v3 whole, which is shorter than its diff:
```python
import jax
import jax.numpy as jnp
from jax import lax
from jax.experimental import pallas as pl
from jax.experimental.pallas import tpu as pltpu
from jax.sharding import PartitionSpec as P

MESH = pl.DeviceIdType.MESH

PAIR_STEPS = [(1, 0)] + [(dx, dz) for dz in (1, 7, 2, 6, 3, 5, 4) for dx in (0, 1)]
RING = (1, 3, 2)
GROUPS = 4
SPAN = 8 // GROUPS
EARLY = 10


def kernel(
    panel_ref,
    amplitude_ref,
    energy_in,
    fock_in,
    occ_in,
    freq_in,
    lmo_in,
    near_in,
    rank_in,
    out_ref,
    pbuf,
    inamp,
    energy_ref,
    fock_ref,
    occ_ref,
    freq_ref,
    lmo_ref,
    near_ref,
    rank_ref,
    mt_ref,
    amp_ref,
    nbr_ref,
    wgt_ref,
    diag,
    flat,
    mbuf,
    abuf,
    nbuf,
    wbuf,
    nsm,
    wsm,
    proj,
    mtr,
    coll,
    sa,
    sb,
    ra,
    rb,
    ta,
    tb,
    ca,
    cb,
    vbuf,
    ubuf,
    fin,
    l_sem,
    a_sem,
    b_sem,
    y_sem,
    d_sem,
    m_send,
    m_recv,
    f_send,
    f_recv,
    n_sem,
    w_sem,
    r_send,
    r_recv,
    t_send,
    t_recv,
    u_sem,
    x_sem,
):
    pair = lax.axis_index("pair")
    aux = lax.axis_index("aux")
    xlo, z = pair // 8, lax.rem(pair, 8)
    chip, core = aux // 2, lax.rem(aux, 2)
    y, xhi = chip // 2, lax.rem(chip, 2)
    x = xhi * 2 + xlo
    other = 1 - core

    def at(xx, yy, zz, cc):
        return (lax.rem(xx, 2) * 8 + zz, (yy * 2 + xx // 2) * 2 + cc)

    partner = at(x, y, z, other)

    def pair_to(step):
        dx, dz = step
        return lax.rem(xlo + dx, 2) * 8 + lax.rem(z + dz, 8)

    def pair_from(step):
        dx, dz = step
        return lax.rem(xlo + dx, 2) * 8 + lax.rem(z + 8 - dz, 8)

    def x_to(d):
        return at(lax.rem(x + d, 4), y, z, core)

    def y_to(d):
        return at(x, lax.rem(y + d, 4), z, core)

    def z_to(d):
        return at(x, y, lax.rem(z + d, 8), core)

    barrier = pltpu.get_barrier_semaphore()

    def greet(target):
        pl.semaphore_signal(barrier, inc=1, device_id=target, device_id_type=MESH)

    for step in PAIR_STEPS:
        greet((pair_to(step), aux))
    for d in RING:
        greet(y_to(d))
    greet(at(lax.rem(xhi + 1, 2) * 2 + xlo, y, z, core))
    greet(at(lax.rem(xhi + 1, 2) * 2 + 1 - xlo, y, z, core))
    greet(partner)

    def remote(src, dst, send, recv, target):
        return pltpu.make_async_remote_copy(
            src_ref=src,
            dst_ref=dst,
            send_sem=send,
            recv_sem=recv,
            device_id=target,
            device_id_type=MESH,
        )

    def arrived(ref, sems, target):
        remote(ref, ref, sems.at[0], sems.at[1], target).wait_recv()

    def left(ref, sems, target):
        remote(ref, ref, sems.at[0], sems.at[1], target).wait_send()

    loads = [
        pltpu.make_async_copy(src, dst, l_sem.at[i])
        for i, (src, dst) in enumerate(
            [
                (panel_ref, pbuf),
                (amplitude_ref, inamp),
                (energy_in, energy_ref),
                (fock_in, fock_ref),
                (occ_in, occ_ref),
                (freq_in, freq_ref),
                (lmo_in, lmo_ref),
                (near_in, near_ref),
                (rank_in, rank_ref),
            ]
        )
    ]
    for load in loads:
        load.start()
    for load in loads[1:]:
        load.wait()
    lane = lax.broadcasted_iota(jnp.int32, (1, 128), 1)
    near_row = jnp.zeros((1, 128), jnp.int32)
    weight_row = jnp.zeros((1, 128), jnp.float32)
    for c in range(2):
        l0, l1 = lmo_ref[0, 2 * pair + c], lmo_ref[1, 2 * pair + c]
        near = [near_ref[c, k] for k in range(8)]
        value = [fock_ref[l0, lmo_ref[0, n]] + fock_ref[l1, lmo_ref[1, n]] for n in near]
        for k in range(8):
            weight = value[k]
            for j in range(k + 1, 8):
                weight = weight + jnp.where(near[j] == near[k], value[j], 0.0)
            for j in range(k):
                weight = jnp.where(near[j] == near[k], 0.0, weight)
            here = lane == c * 8 + k
            near_row = jnp.where(here, near[k], near_row)
            weight_row = jnp.where(here, weight, weight_row)
    weight_row = weight_row.astype(jnp.bfloat16).astype(jnp.float32)
    nbr_ref[...] = near_row
    wgt_ref[...] = weight_row
    nbuf[pair] = near_row
    wbuf[pair] = weight_row
    slot_row = lax.broadcasted_iota(jnp.int32, (16, 120), 0)
    slot_col = lax.broadcasted_iota(jnp.int32, (16, 120), 1)
    pick = ((slot_row < 15) & (slot_col == chip * 15 + slot_row)).astype(jnp.float32)
    pick16 = pick.astype(jnp.bfloat16)
    amp_ref[...] = jnp.zeros_like(amp_ref)
    for s in range(2):
        rows = jnp.dot(pick16, inamp[core, s], preferred_element_type=jnp.float32)
        amp_ref[:, s * 128 : s * 128 + 120] = rows.astype(jnp.bfloat16)
    abuf[chip, core, pair] = amp_ref[...]
    loads[0].wait()
    place_row = lax.broadcasted_iota(jnp.int32, (128, 120), 0)
    place_col = lax.broadcasted_iota(jnp.int32, (128, 120), 1)
    fill = lax.rem(place_row, 16)
    source = place_row // 16 * 15 + fill
    for c in range(2):
        keep = (fill < 15) & (source == place_col) & (place_col < rank_ref[c])
        place = keep.astype(jnp.float32).astype(jnp.bfloat16)
        for t in range(9):
            cols = pl.ds(t * 256, 256)
            moved = jnp.dot(place, pbuf[c, :, cols], preferred_element_type=jnp.float32)
            mt_ref[c, cols, :] = moved.astype(jnp.bfloat16).T
    pl.semaphore_wait(barrier, 21)

    def m_rows(p):
        return mt_ref.at[:, pl.ds(pl.multiple_of(p * 144, 16), 144), :]

    for dz in (1, 7, 2, 6, 3, 5, 4):
        remote(amp_ref, abuf.at[chip, core, pair], a_sem.at[0], a_sem.at[1], z_to(dz)).start()
    for i, step in enumerate(PAIR_STEPS):
        p = pair_to(step)
        remote(m_rows(p), mbuf.at[pair, core], m_send, m_recv.at[i], (p, aux)).start()
    remote(m_rows(pair), mbuf.at[pair, core], f_send, f_recv.at[15], partner).start()
    for i, step in enumerate(PAIR_STEPS):
        to = (pair_to(step), aux)
        remote(nbr_ref, nbuf.at[pair], n_sem.at[0], n_sem.at[1], to).start()
        remote(wgt_ref, wbuf.at[pair], w_sem.at[0], w_sem.at[1], to).start()
    mbuf[pair, core] = mt_ref[:, pl.ds(pl.multiple_of(pair * 144, 16), 144), :]
    diag[...] = jnp.zeros_like(diag)
    for c in range(2):
        across = energy_ref[pl.ds(c, 1), :]
        down = jnp.sum(pick * across, axis=1, keepdims=True)
        occ = occ_ref[lmo_ref[0, 2 * pair + c]] + occ_ref[lmo_ref[1, 2 * pair + c]]
        shift = down + across - occ
        for s in range(2):
            rows = jnp.dot(pick16, inamp[c, s], preferred_element_type=jnp.float32)
            sign = 1.0 - 2.0 * s
            diag[c, s, :, :120] = (shift - sign * freq_ref[0]) * rows

    def relay_block(i):
        step = PAIR_STEPS[i]
        p = pair_from(step)
        block = mbuf.at[p, core]
        remote(block, block, m_send, m_recv.at[i], (p, aux)).wait_recv()
        remote(block, block, f_send, f_recv.at[i], partner).start()

    def relayed(i):
        p = pair if i == 15 else pair_from(PAIR_STEPS[i])
        block = mbuf.at[p, other]
        remote(block, block, f_send, f_recv.at[i], partner).wait_recv()
        for h in range(2):
            mtr[p, h] = mbuf[p, h, core].T
        return p

    def project(p):
        for c in range(2):
            matrix = abuf[:, c, p].reshape(128, 256)
            for h in range(2):
                proj[2 * p + c, h] = jnp.dot(
                    mbuf[p, h, c], matrix, preferred_element_type=jnp.float32
                ).astype(jnp.bfloat16)

    def column(xx):
        return abuf.at[y * 2 + xx // 2, core, pl.ds(lax.rem(xx, 2) * 8, 8)]

    def rows_of(yy, cc):
        return abuf.at[pl.ds(yy * 2, 2), cc]

    relayed(15)
    relay_block(0)
    relay_block(1)
    arrived(abuf.at[0, 0, pl.ds(0, 7)], a_sem, partner)
    for d in RING:
        remote(column(x), column(x), b_sem.at[0], b_sem.at[1], x_to(d)).start()
    for d in RING:
        remote(column(x), column(x), y_sem.at[0], y_sem.at[1], y_to(d)).start()
    relay_block(2)
    relayed(0)
    relayed(1)
    arrived(abuf.at[pl.ds(0, 3), 0, pl.ds(0, 8)], b_sem, partner)
    for e in RING:
        for d in RING:
            xx = lax.rem(x + e, 4)
            remote(column(xx), column(xx), y_sem.at[0], y_sem.at[1], y_to(d)).start()
    remote(rows_of(y, core), rows_of(y, core), d_sem.at[0], d_sem.at[1], partner).start()
    for i in range(3, EARLY):
        relay_block(i)
        relayed(i - 1)
    arrived(abuf.at[pl.ds(0, 6), 0], y_sem, partner)
    for d in RING:
        yy = lax.rem(y + d, 4)
        remote(rows_of(yy, core), rows_of(yy, core), d_sem.at[0], d_sem.at[1], partner).start()
    relayed(EARLY - 1)
    relay_block(EARLY)
    arrived(nbuf.at[pl.ds(0, 15)], n_sem, partner)
    arrived(wbuf.at[pl.ds(0, 15)], w_sem, partner)
    to_nsm = pltpu.make_async_copy(nbuf, nsm, l_sem.at[0])
    to_wsm = pltpu.make_async_copy(wbuf, wsm, l_sem.at[1])
    to_nsm.start()
    to_wsm.start()
    to_nsm.wait()
    to_wsm.wait()
    arrived(abuf.at[:, 0], d_sem, partner)
    project(pair)
    for i in range(EARLY):
        project(pair_from(PAIR_STEPS[i]))
    for i in range(EARLY, 15):
        if i + 1 < 15:
            relay_block(i + 1)
        project(relayed(i))

    def close(lo, zz):
        p = lo * 8 + zz
        for h in range(2):
            total = jnp.zeros((144, 256), jnp.float32)
            for k in range(8):
                n = nsm[p, 0, core * 8 + k]
                w = wsm[p, 0, core * 8 + k]
                total = total + w * proj[n, h].astype(jnp.float32)
            coll[lo, h] = total.astype(jnp.bfloat16)
        closed = jnp.dot(mtr[p, 0], coll[lo, 0], preferred_element_type=jnp.float32)
        closed = closed + jnp.dot(mtr[p, 1], coll[lo, 1], preferred_element_type=jnp.float32)
        closed = closed.astype(jnp.bfloat16).reshape(4, 2, 16, 256)
        sa[:, :, lo, zz] = closed[:, :, :, :128]
        for hi in range(2):
            sb[hi, lo, :, zz] = closed[:, hi, :, 128:]

    def close_both(zz, carry):
        close(0, zz)
        close(1, zz)
        return carry

    def span(q):
        return pl.ds(q * SPAN, SPAN)

    for q in range(GROUPS):
        lax.fori_loop(q * SPAN, (q + 1) * SPAN, close_both, 0)
        for i, d in enumerate(RING):
            yy, xx = lax.rem(y + d, 4), lax.rem(x + d, 4)
            remote(
                sa.at[yy, :, :, span(q)],
                ra.at[i, :, :, span(q)],
                r_send.at[0],
                r_recv.at[0, q],
                y_to(d),
            ).start()
            remote(
                sb.at[xx // 2, lax.rem(xx, 2), :, span(q)],
                rb.at[i, :, span(q)],
                r_send.at[1],
                r_recv.at[1, q],
                x_to(d),
            ).start()

    def first_sum(q):
        part = ra.at[:, :, :, span(q)]
        remote(part, part, r_send.at[0], r_recv.at[0, q], partner).wait_recv()
        total = sa[y, :, :, span(q)].astype(jnp.float32)
        for i in range(3):
            total = total + ra[i, :, :, span(q)].astype(jnp.float32)
        ta[:, :, span(q)] = total.astype(jnp.bfloat16)
        for i, d in enumerate(RING):
            xx = lax.rem(x + d, 4)
            remote(
                ta.at[xx // 2, lax.rem(xx, 2), span(q)],
                ca.at[i, span(q)],
                t_send.at[0],
                t_recv.at[0, q],
                x_to(d),
            ).start()
        part = rb.at[:, :, span(q)]
        remote(part, part, r_send.at[1], r_recv.at[1, q], partner).wait_recv()
        total = sb[xhi, xlo, :, span(q)].astype(jnp.float32)
        for i in range(3):
            total = total + rb[i, :, span(q)].astype(jnp.float32)
        tb[:, span(q)] = total.astype(jnp.bfloat16)
        for i, d in enumerate(RING):
            yy = lax.rem(y + d, 4)
            remote(
                tb.at[yy, span(q)],
                cb.at[i, span(q)],
                t_send.at[1],
                t_recv.at[1, q],
                y_to(d),
            ).start()

    def second_sum(q):
        part = ca.at[:, span(q)]
        remote(part, part, t_send.at[0], t_recv.at[0, q], partner).wait_recv()
        total = ta[xhi, xlo, span(q)].astype(jnp.float32)
        for i in range(3):
            total = total + ca[i, span(q)].astype(jnp.float32)
        vbuf[span(q), 0] = total.astype(jnp.bfloat16)
        part = cb.at[:, span(q)]
        remote(part, part, t_send.at[1], t_recv.at[1, q], partner).wait_recv()
        total = tb[y, span(q)].astype(jnp.float32)
        for i in range(3):
            total = total + cb[i, span(q)].astype(jnp.float32)
        vbuf[span(q), 1] = total.astype(jnp.bfloat16)
        for j in range(SPAN):
            zz = q * SPAN + j

            @pl.when(zz != z)
            def _():
                slot = lax.rem(zz - z + 8, 8) - 1
                remote(
                    vbuf.at[zz], ubuf.at[slot], u_sem.at[0], u_sem.at[1], at(x, y, zz, core)
                ).start()

    first_sum(0)
    for q in range(1, GROUPS):
        first_sum(q)
        second_sum(q - 1)
    second_sum(GROUPS - 1)
    arrived(ubuf, u_sem, partner)
    total = vbuf[z].astype(jnp.float32)
    for slot in range(7):
        total = total + ubuf[slot].astype(jnp.float32)
    fin[core] = total
    swap = remote(fin.at[core], fin.at[core], x_sem.at[0], x_sem.at[1], partner)
    swap.start()
    remote(fin.at[other], fin.at[other], x_sem.at[0], x_sem.at[1], partner).wait_recv()
    for c in range(2):
        for s in range(2):
            rows = fin[c, s] + diag[c, s]
            line = slice(2 * c + s, 2 * c + s + 1)
            for j in range(8):
                row = jnp.where(core == 0, rows[j : j + 1, :120], rows[j + 7 : j + 8, :120])
                flat[line, j * 120 : j * 120 + 120] = row
            whole = flat[line, :]
            out_ref[c, s : s + 1, :] = jnp.where(core == 0, whole[:, :900], whole[:, 60:960])
    left(abuf.at[0, 0, pl.ds(0, 7)], a_sem, partner)
    left(abuf.at[pl.ds(0, 3), 0, pl.ds(0, 8)], b_sem, partner)
    left(abuf.at[pl.ds(0, 6), 0], y_sem, partner)
    left(abuf.at[:, 0], d_sem, partner)
    left(nbuf.at[pl.ds(0, 15)], n_sem, partner)
    left(wbuf.at[pl.ds(0, 15)], w_sem, partner)
    left(ubuf, u_sem, partner)
    blocks = mbuf.at[pl.ds(0, 15), 0]
    remote(blocks, blocks, m_send, m_recv.at[0], partner).wait_send()
    blocks = mbuf.at[:, 0]
    remote(blocks, blocks, f_send, f_recv.at[0], partner).wait_send()
    for half, (one, two) in enumerate([(ra, ca), (rb, cb)]):
        remote(one, one, r_send.at[half], r_recv.at[half, 0], partner).wait_send()
        remote(two, two, t_send.at[half], t_recv.at[half, 0], partner).wait_send()
    swap.wait_send()


def coupled_rows(*operands):
    bf16, f32, i32 = jnp.bfloat16, jnp.float32, jnp.int32
    dma = pltpu.SemaphoreType.DMA
    vmem, hbm = pl.BlockSpec(memory_space=pltpu.VMEM), pl.BlockSpec(memory_space=pl.ANY)
    return pl.pallas_call(
        kernel,
        out_shape=jax.ShapeDtypeStruct((2, 2, 900), f32),
        in_specs=[hbm] * 9,
        out_specs=vmem,
        scratch_shapes=[
            pltpu.VMEM((2, 120, 2304), bf16),
            pltpu.VMEM((2, 2, 120, 120), bf16),
            pltpu.VMEM((2, 120), f32),
            pltpu.SMEM((64, 64), f32),
            pltpu.SMEM((64,), f32),
            pltpu.SMEM((1,), f32),
            pltpu.SMEM((2, 32), i32),
            pltpu.SMEM((2, 8), i32),
            pltpu.SMEM((2,), i32),
            pltpu.VMEM((2, 2304, 128), bf16),
            pltpu.VMEM((16, 256), bf16),
            pltpu.VMEM((1, 128), i32),
            pltpu.VMEM((1, 128), f32),
            pltpu.VMEM((2, 2, 16, 128), f32),
            pltpu.VMEM((4, 1024), f32),
            pltpu.VMEM((16, 2, 2, 144, 128), bf16),
            pltpu.VMEM((8, 2, 16, 16, 256), bf16),
            pltpu.VMEM((16, 1, 128), i32),
            pltpu.VMEM((16, 1, 128), f32),
            pltpu.SMEM((16, 1, 128), i32),
            pltpu.SMEM((16, 1, 128), f32),
            pltpu.VMEM((32, 2, 144, 256), bf16),
            pltpu.VMEM((16, 2, 128, 144), bf16),
            pltpu.VMEM((2, 2, 144, 256), bf16),
            pltpu.VMEM((4, 2, 2, 8, 16, 128), bf16),
            pltpu.VMEM((2, 2, 4, 8, 16, 128), bf16),
            pltpu.VMEM((3, 2, 2, 8, 16, 128), bf16),
            pltpu.VMEM((3, 4, 8, 16, 128), bf16),
            pltpu.VMEM((2, 2, 8, 16, 128), bf16),
            pltpu.VMEM((4, 8, 16, 128), bf16),
            pltpu.VMEM((3, 8, 16, 128), bf16),
            pltpu.VMEM((3, 8, 16, 128), bf16),
            pltpu.VMEM((8, 2, 16, 128), bf16),
            pltpu.VMEM((7, 2, 16, 128), bf16),
            pltpu.VMEM((2, 2, 16, 128), f32),
            dma((9,)),
            dma((2,)),
            dma((2,)),
            dma((2,)),
            dma((2,)),
            dma,
            dma((15,)),
            dma,
            dma((16,)),
            dma((2,)),
            dma((2,)),
            dma((2,)),
            dma((2, GROUPS)),
            dma((2,)),
            dma((2, GROUPS)),
            dma((2,)),
            dma((2,)),
        ],
        compiler_params=pltpu.CompilerParams(
            collective_id=0, has_side_effects=True, vmem_limit_bytes=56 << 20
        ),
        name="coupled_rows",
    )(*operands)


def body(
    panels,
    amplitudes,
    drive,
    pno_energy,
    occ_energy,
    frequency,
    pair_lmo,
    neighbours,
    pno_ranks,
    fock_off,
):
    return drive + coupled_rows(
        panels,
        amplitudes,
        pno_energy,
        fock_off,
        occ_energy,
        frequency,
        pair_lmo.T,
        neighbours,
        pno_ranks,
    )


def solution(mesh):
    placed = (
        P("pair", None, "aux"),
        P("pair", None, None, None),
        P("pair", None, "aux"),
        P("pair", None),
        P(),
        P(),
        P(),
        P("pair", None),
        P("pair"),
        P(),
    )
    return jax.shard_map(
        body, mesh=mesh, in_specs=placed, out_specs=P("pair", None, "aux"), check_vma=False
    )
```

time: 167 us -> 65.6 us (0.39)
  Pallas kernels: 0 us -> 63.3 us
  blocking collectives: 54.4 us -> 0 us
  waiting for transfers between devices: 46.9 us -> 0 us
  starting transfers between devices: 27.7 us -> 0 us
  between operations: 14.2 us -> 0.68 us
  local copies, waits for them, and re-layouts: 13.3 us -> 0.01 us
  matrix products: 6.18 us -> 0 us
  other arithmetic: 4.18 us -> 1.33 us
    pallas_call x0 -> x1, Pallas kernels: none -> 63.3 us  [coupled_rows(): pl.pallas_call(kernel, out_shape=jax.ShapeDtypeStruct((2, 2, 900), f32),...]
    all_gather x1 -> x0, blocking collectives: 54.4 us -> none  [body(): all_weights = lax.all_gather(weights, 'pair', axis=0, tiled=True)]
    all_to_all x3 -> x0, waiting for transfers between devices: 34.2 us -> none  [the longest x2 34.2 us: sent_and_summed(): lax.all_to_all(cut_along(shard, dim, length), axis, 0, 0, tiled=True)]
    all_to_all x3 -> x0, starting transfers between devices: 27.7 us -> none  [the longest x2 17.7 us: sent_and_summed(): lax.all_to_all(cut_along(shard, dim, length), axis, 0, 0, tiled=True)]
    all_gather x1 -> x0, waiting for transfers between devices: 12 us -> none  [body(): all_amps = lax.all_gather(amplitudes, 'pair', axis=0, tiled=True)]
    dot_general x5 -> x0, matrix products: 6.18 us -> none  [the longest x1 2.39 us: body(): jnp.einsum('paq,psqc->psac', slices, collected, preferred_element_type=jn...]
    transpose x2 -> x0, local copies, waits for them, and re-layouts: 4.61 us -> none  [cut_along(): return jnp.moveaxis(shard.reshape(*before, length, -1, *after), dim, 0)]
    another operation x1 -> x0, local copies, waits for them, and re-layouts: 3.56 us -> none  [cut_along(): return jnp.moveaxis(shard.reshape(*before, length, -1, *after), dim, 0)]
  transfers between devices with their start and end apart: 4 -> 0, of which waited for: 3 -> 0; matrix products, arithmetic and copies ran while one was open for 3% -> 0% of each run, Pallas kernels for 0% -> 0%
where the time goes in v3:
time: 65.6 us; the launch traced here: 65.4 us
  Pallas kernels  63.3 us (96%)
  other arithmetic  1.33 us (2%)
  between operations  0.68 us (1%)
    pallas_call x1, Pallas kernels, coupled_rows(): pl.pallas_call(kernel, out_shape=jax.ShapeDtypeStruct((2, 2, 900), f32),...  63.3 us
    add x1, other arithmetic, body(): drive + coupled_rows(panels, amplitudes, pno_energy, fock_off, occ_energy...  1.33 us

profile of v3, /device:TPU:1, one launch (start us, length us, event | category | flops | bytes accessed | tf_op | source)
XLA Modules:
  0.0 65.4 jit_solution(11825553167871007815)
XLA Ops:
  0.0 0.0 copy-start
  0.7 63.3 %coupled_rows.1 = f32[2,2,900]{2,1,0:T(2,128)} custom-call(bf16[2,120,2304]{2,1,0:T(8,128)(2,1)} %panel_ref.1, bf16[2,2,120,120]{3,2,1,0:T(8,128)(2,1)} %amplitude_ref.1, f32[2,120]{1,0:T(2,128)} %energy_in.1, f32[64,64]{1,0:T(8,128)} %fock_in.1, f32[64]{0:T(128)} %occ_in.1, f32[1]{0:T(128)S(6)} %copy.11.freq_in, s32[2,32]{1,0:T(2,128)} %bitcast.1, ...), custom_call_target="tpu_custom_call" | custom-call | tf_op jit(solution)/shard_map/coupled_rows/pallas_call | solution.py:442
  64.0 0.0 copy-done
  64.0 1.3 %add.3 = f32[2,2,900]{2,1,0:T(2,128)} add(f32[2,2,900]{2,1,0:T(2,128)S(1)} %copy-done, f32[2,2,900]{2,1,0:T(2,128)} %coupled_rows.1) | non-fusion elementwise | flops 3600 | bytes 43200 | tf_op jit(solution)/shard_map/add | solution.py:520
Async XLA Ops:
  0.0 64.0 %copy-start = (f32[2,2,900]{2,1,0:T(2,128)S(1)}, f32[2,2,900]{2,1,0:T(2,128)}, u32[]{:S(2)}) copy-start(f32[2,2,900]{2,1,0:T(2,128)} %param.12) | copy-start | bytes 43204

commit v4 on v3

--- a/solution.py
+++ b/solution.py
@@ -59,7 +59,6 @@
     cb,
     vbuf,
     ubuf,
-    fin,
     l_sem,
     a_sem,
     b_sem,
@@ -76,7 +75,6 @@
     t_send,
     t_recv,
     u_sem,
-    x_sem,
 ):
     pair = lax.axis_index("pair")
     aux = lax.axis_index("aux")
@@ -120,6 +118,8 @@
     greet(at(lax.rem(xhi + 1, 2) * 2 + xlo, y, z, core))
     greet(at(lax.rem(xhi + 1, 2) * 2 + 1 - xlo, y, z, core))
     greet(partner)
+    for dz in range(1, 8):
+        greet(at(x, y, lax.rem(z + dz, 8), other))
 
     def remote(src, dst, send, recv, target):
         return pltpu.make_async_remote_copy(
@@ -199,30 +199,34 @@
             cols = pl.ds(t * 256, 256)
             moved = jnp.dot(place, pbuf[c, :, cols], preferred_element_type=jnp.float32)
             mt_ref[c, cols, :] = moved.astype(jnp.bfloat16).T
-    pl.semaphore_wait(barrier, 21)
+    pl.semaphore_wait(barrier, 28)
 
     def m_rows(p):
         return mt_ref.at[:, pl.ds(pl.multiple_of(p * 144, 16), 144), :]
 
     for dz in (1, 7, 2, 6, 3, 5, 4):
         remote(amp_ref, abuf.at[chip, core, pair], a_sem.at[0], a_sem.at[1], z_to(dz)).start()
+    for i, step in enumerate(PAIR_STEPS):
+        to = (pair_to(step), aux)
+        remote(nbr_ref, nbuf.at[pair], n_sem.at[0], n_sem.at[1], to).start()
+        remote(wgt_ref, wbuf.at[pair], w_sem.at[0], w_sem.at[1], to).start()
     for i, step in enumerate(PAIR_STEPS):
         p = pair_to(step)
         remote(m_rows(p), mbuf.at[pair, core], m_send, m_recv.at[i], (p, aux)).start()
     remote(m_rows(pair), mbuf.at[pair, core], f_send, f_recv.at[15], partner).start()
-    for i, step in enumerate(PAIR_STEPS):
-        to = (pair_to(step), aux)
-        remote(nbr_ref, nbuf.at[pair], n_sem.at[0], n_sem.at[1], to).start()
-        remote(wgt_ref, wbuf.at[pair], w_sem.at[0], w_sem.at[1], to).start()
     mbuf[pair, core] = mt_ref[:, pl.ds(pl.multiple_of(pair * 144, 16), 144), :]
     diag[...] = jnp.zeros_like(diag)
+    own_row = lax.broadcasted_iota(jnp.int32, (8, 120), 0) + chip * 15 + core * 7
+    own = (lax.broadcasted_iota(jnp.int32, (8, 120), 1) == own_row).astype(jnp.float32)
     for c in range(2):
         across = energy_ref[pl.ds(c, 1), :]
-        down = jnp.sum(pick * across, axis=1, keepdims=True)
+        down = jnp.sum(own * across, axis=1, keepdims=True)
         occ = occ_ref[lmo_ref[0, 2 * pair + c]] + occ_ref[lmo_ref[1, 2 * pair + c]]
         shift = down + across - occ
         for s in range(2):
-            rows = jnp.dot(pick16, inamp[c, s], preferred_element_type=jnp.float32)
+            rows = jnp.dot(
+                own.astype(jnp.bfloat16), inamp[c, s], preferred_element_type=jnp.float32
+            )
             sign = 1.0 - 2.0 * s
             diag[c, s, :, :120] = (shift - sign * freq_ref[0]) * rows
 
@@ -245,9 +249,8 @@
         for c in range(2):
             matrix = abuf[:, c, p].reshape(128, 256)
             for h in range(2):
-                proj[2 * p + c, h] = jnp.dot(
-                    mbuf[p, h, c], matrix, preferred_element_type=jnp.float32
-                ).astype(jnp.bfloat16)
+                block = jnp.dot(mbuf[p, h, c], matrix, preferred_element_type=jnp.float32)
+                proj[2 * p + c, h] = block.astype(jnp.bfloat16).astype(jnp.float32)
 
     def column(xx):
         return abuf.at[y * 2 + xx // 2, core, pl.ds(lax.rem(xx, 2) * 8, 8)]
@@ -305,7 +308,7 @@
             for k in range(8):
                 n = nsm[p, 0, core * 8 + k]
                 w = wsm[p, 0, core * 8 + k]
-                total = total + w * proj[n, h].astype(jnp.float32)
+                total = total + w * proj[n, h]
             coll[lo, h] = total.astype(jnp.bfloat16)
         closed = jnp.dot(mtr[p, 0], coll[lo, 0], preferred_element_type=jnp.float32)
         closed = closed + jnp.dot(mtr[p, 1], coll[lo, 1], preferred_element_type=jnp.float32)
@@ -379,21 +382,34 @@
         total = ta[xhi, xlo, span(q)].astype(jnp.float32)
         for i in range(3):
             total = total + ca[i, span(q)].astype(jnp.float32)
-        vbuf[span(q), 0] = total.astype(jnp.bfloat16)
+        vbuf[span(q), 0, 0] = total[:, :8].astype(jnp.bfloat16)
+        vbuf[span(q), 1, 0] = total[:, 7:15].astype(jnp.bfloat16)
         part = cb.at[:, span(q)]
         remote(part, part, t_send.at[1], t_recv.at[1, q], partner).wait_recv()
         total = tb[y, span(q)].astype(jnp.float32)
         for i in range(3):
             total = total + cb[i, span(q)].astype(jnp.float32)
-        vbuf[span(q), 1] = total.astype(jnp.bfloat16)
+        vbuf[span(q), 0, 1] = total[:, :8].astype(jnp.bfloat16)
+        vbuf[span(q), 1, 1] = total[:, 7:15].astype(jnp.bfloat16)
         for j in range(SPAN):
             zz = q * SPAN + j
+            slot = lax.rem(zz - z + 8, 8)
+            remote(
+                vbuf.at[zz, other],
+                ubuf.at[slot * 2 + core],
+                u_sem.at[0],
+                u_sem.at[1],
+                at(x, y, zz, other),
+            ).start()
 
             @pl.when(zz != z)
             def _():
-                slot = lax.rem(zz - z + 8, 8) - 1
                 remote(
-                    vbuf.at[zz], ubuf.at[slot], u_sem.at[0], u_sem.at[1], at(x, y, zz, core)
+                    vbuf.at[zz, core],
+                    ubuf.at[slot * 2 + core],
+                    u_sem.at[0],
+                    u_sem.at[1],
+                    at(x, y, zz, core),
                 ).start()
 
     first_sum(0)
@@ -401,21 +417,16 @@
         first_sum(q)
         second_sum(q - 1)
     second_sum(GROUPS - 1)
-    arrived(ubuf, u_sem, partner)
-    total = vbuf[z].astype(jnp.float32)
-    for slot in range(7):
-        total = total + ubuf[slot].astype(jnp.float32)
-    fin[core] = total
-    swap = remote(fin.at[core], fin.at[core], x_sem.at[0], x_sem.at[1], partner)
-    swap.start()
-    remote(fin.at[other], fin.at[other], x_sem.at[0], x_sem.at[1], partner).wait_recv()
+    ubuf[core] = vbuf[z, core]
+    arrived(ubuf.at[pl.ds(0, 15)], u_sem, partner)
     for c in range(2):
+        total = diag[c]
+        for slot in range(8):
+            total = total + ubuf[slot * 2 + c].astype(jnp.float32)
         for s in range(2):
-            rows = fin[c, s] + diag[c, s]
             line = slice(2 * c + s, 2 * c + s + 1)
             for j in range(8):
-                row = jnp.where(core == 0, rows[j : j + 1, :120], rows[j + 7 : j + 8, :120])
-                flat[line, j * 120 : j * 120 + 120] = row
+                flat[line, j * 120 : j * 120 + 120] = total[s, j : j + 1, :120]
             whole = flat[line, :]
             out_ref[c, s : s + 1, :] = jnp.where(core == 0, whole[:, :900], whole[:, 60:960])
     left(abuf.at[0, 0, pl.ds(0, 7)], a_sem, partner)
@@ -424,7 +435,7 @@
     left(abuf.at[:, 0], d_sem, partner)
     left(nbuf.at[pl.ds(0, 15)], n_sem, partner)
     left(wbuf.at[pl.ds(0, 15)], w_sem, partner)
-    left(ubuf, u_sem, partner)
+    left(ubuf.at[pl.ds(0, 15)], u_sem, partner)
     blocks = mbuf.at[pl.ds(0, 15), 0]
     remote(blocks, blocks, m_send, m_recv.at[0], partner).wait_send()
     blocks = mbuf.at[:, 0]
@@ -432,13 +443,12 @@
     for half, (one, two) in enumerate([(ra, ca), (rb, cb)]):
         remote(one, one, r_send.at[half], r_recv.at[half, 0], partner).wait_send()
         remote(two, two, t_send.at[half], t_recv.at[half, 0], partner).wait_send()
-    swap.wait_send()
 
 
 def coupled_rows(*operands):
     bf16, f32, i32 = jnp.bfloat16, jnp.float32, jnp.int32
     dma = pltpu.SemaphoreType.DMA
-    vmem, hbm = pl.BlockSpec(memory_space=pltpu.VMEM), pl.BlockSpec(memory_space=pl.ANY)
+    vmem, hbm = pl.BlockSpec(memory_space=pltpu.VMEM), pl.BlockSpec(memory_space=pltpu.HBM)
     return pl.pallas_call(
         kernel,
         out_shape=jax.ShapeDtypeStruct((2, 2, 900), f32),
@@ -458,7 +468,7 @@
             pltpu.VMEM((16, 256), bf16),
             pltpu.VMEM((1, 128), i32),
             pltpu.VMEM((1, 128), f32),
-            pltpu.VMEM((2, 2, 16, 128), f32),
+            pltpu.VMEM((2, 2, 8, 128), f32),
             pltpu.VMEM((4, 1024), f32),
             pltpu.VMEM((16, 2, 2, 144, 128), bf16),
             pltpu.VMEM((8, 2, 16, 16, 256), bf16),
@@ -466,7 +476,7 @@
             pltpu.VMEM((16, 1, 128), f32),
             pltpu.SMEM((16, 1, 128), i32),
             pltpu.SMEM((16, 1, 128), f32),
-            pltpu.VMEM((32, 2, 144, 256), bf16),
+            pltpu.VMEM((32, 2, 144, 256), f32),
             pltpu.VMEM((16, 2, 128, 144), bf16),
             pltpu.VMEM((2, 2, 144, 256), bf16),
             pltpu.VMEM((4, 2, 2, 8, 16, 128), bf16),
@@ -477,9 +487,8 @@
             pltpu.VMEM((4, 8, 16, 128), bf16),
             pltpu.VMEM((3, 8, 16, 128), bf16),
             pltpu.VMEM((3, 8, 16, 128), bf16),
-            pltpu.VMEM((8, 2, 16, 128), bf16),
-            pltpu.VMEM((7, 2, 16, 128), bf16),
-            pltpu.VMEM((2, 2, 16, 128), f32),
+            pltpu.VMEM((8, 2, 2, 8, 128), bf16),
+            pltpu.VMEM((16, 2, 8, 128), bf16),
             dma((9,)),
             dma((2,)),
             dma((2,)),
@@ -496,13 +505,12 @@
             dma((2,)),
             dma((2, GROUPS)),
             dma((2,)),
-            dma((2,)),
         ],
         compiler_params=pltpu.CompilerParams(
-            collective_id=0, has_side_effects=True, vmem_limit_bytes=56 << 20
+            collective_id=0, has_side_effects=True, vmem_limit_bytes=28 << 20
         ),
         name="coupled_rows",
-    )(*operands)
+    )(*[o if o.size == 1 else pltpu.with_memory_space_constraint(o, pltpu.HBM) for o in operands])
 
 
 def body(

time: 65.6 us -> 59 us (0.90)
  Pallas kernels: 63.3 us -> 57.6 us
  other arithmetic: 1.33 us -> 0.62 us
    pallas_call x1, Pallas kernels: 63.3 us -> 57.6 us  [coupled_rows(): pl.pallas_call(kernel, out_shape=jax.ShapeDtypeStruct((2, 2, 900), f32),...]
    add x1, other arithmetic: 1.33 us -> 0.62 us  [body(): drive + coupled_rows(panels, amplitudes, pno_energy, fock_off, occ_energy...]
where the time goes in v4:
time: 59 us; the launch traced here: 58.9 us
  Pallas kernels  57.6 us (98%)
  between operations  0.68 us (1%)
  other arithmetic  0.62 us (1%)
    pallas_call x1, Pallas kernels, coupled_rows(): pl.pallas_call(kernel, out_shape=jax.ShapeDtypeStruct((2, 2, 900), f32),...  57.6 us

profile of v4, /device:TPU:1, one launch (start us, length us, event | category | flops | bytes accessed | tf_op | source)
XLA Modules:
  0.0 58.9 jit_solution(1943076345014850432)
XLA Ops:
  0.0 0.0 copy-start
  0.7 57.6 %coupled_rows.1 = f32[2,2,900]{2,1,0:T(2,128)S(1)} custom-call(bf16[2,120,2304]{2,1,0:T(8,128)(2,1)} %panel_ref.1, bf16[2,2,120,120]{3,2,1,0:T(8,128)(2,1)} %amplitude_ref.1, f32[2,120]{1,0:T(2,128)} %energy_in.1, f32[64,64]{1,0:T(8,128)} %fock_in.1, f32[64]{0:T(128)} %occ_in.1, f32[1]{0:T(128)S(6)} %copy.11.freq_in, s32[2,32]{1,0:T(2,128)} %bitcast.1, ...), custom_call_target="tpu_custom_call" | custom-call | tf_op jit(solution)/shard_map/coupled_rows/pallas_call | solution.py:452
  58.2 0.0 copy-done
  58.3 0.6 %add.3 = f32[2,2,900]{2,1,0:T(2,128)} add(f32[2,2,900]{2,1,0:T(2,128)S(1)} %copy-done, f32[2,2,900]{2,1,0:T(2,128)S(1)} %coupled_rows.1) | non-fusion elementwise | flops 3600 | bytes 43200 | tf_op jit(solution)/shard_map/add | solution.py:528
Async XLA Ops:
  0.0 58.2 %copy-start = (f32[2,2,900]{2,1,0:T(2,128)S(1)}, f32[2,2,900]{2,1,0:T(2,128)}, u32[]{:S(2)}) copy-start(f32[2,2,900]{2,1,0:T(2,128)} %param.12) | copy-start | bytes 43204

commit v5 on v4

--- a/solution.py
+++ b/solution.py
@@ -7,11 +7,15 @@
 
 MESH = pl.DeviceIdType.MESH
 
-PAIR_STEPS = [(1, 0)] + [(dx, dz) for dz in (1, 7, 2, 6, 3, 5, 4) for dx in (0, 1)]
+PAIR_STEPS = [(0, dz) for dz in (1, 7, 2, 6, 3, 5, 4)]
+PAIR_STEPS += [(1, dz) for dz in (0, 1, 7, 2, 6, 3, 5, 4)]
+NEAR = 7
 RING = (1, 3, 2)
 GROUPS = 4
 SPAN = 8 // GROUPS
 EARLY = 10
+LAG = 2
+Z_ORDER = (0, 1, 7, 2, 6, 3, 5, 4)
 
 
 def kernel(
@@ -40,7 +44,9 @@
     wgt_ref,
     diag,
     flat,
+    mw,
     mbuf,
+    nb,
     abuf,
     nbuf,
     wbuf,
@@ -155,7 +161,79 @@
     ]
     for load in loads:
         load.start()
-    for load in loads[1:]:
+    loads[1].wait()
+    loads[8].wait()
+    slot_row = lax.broadcasted_iota(jnp.int32, (16, 120), 0)
+    slot_col = lax.broadcasted_iota(jnp.int32, (16, 120), 1)
+    pick = ((slot_row < 15) & (slot_col == chip * 15 + slot_row)).astype(jnp.float32)
+    pick16 = pick.astype(jnp.bfloat16)
+    amp_ref[...] = jnp.zeros_like(amp_ref)
+    for s in range(2):
+        rows = jnp.dot(pick16, inamp[core, s], preferred_element_type=jnp.float32)
+        amp_ref[:, s * 128 : s * 128 + 120] = rows.astype(jnp.bfloat16)
+    abuf[chip, core, pair] = amp_ref[...]
+    loads[0].wait()
+    place_row = lax.broadcasted_iota(jnp.int32, (128, 120), 0)
+    place_col = lax.broadcasted_iota(jnp.int32, (128, 120), 1)
+    fill = lax.rem(place_row, 16)
+    source = place_row // 16 * 15 + fill
+    for c in range(2):
+        keep = (fill < 15) & (source == place_col) & (place_col < rank_ref[c])
+        place = keep.astype(jnp.float32).astype(jnp.bfloat16)
+        for t in range(9):
+            cols = pl.ds(t * 256, 256)
+            moved = jnp.dot(place, pbuf[c, :, cols], preferred_element_type=jnp.float32)
+            mt_ref[c, cols, :] = moved.astype(jnp.bfloat16).T
+    pl.semaphore_wait(barrier, 28)
+
+    spare_row = lax.broadcasted_iota(jnp.int32, (16, 128), 0)
+    spare_col = lax.broadcasted_iota(jnp.int32, (16, 128), 1)
+    last = lax.rem(spare_col, 16) == 15
+
+    def spare(first):
+        hit = last & (spare_col // 16 == spare_row - first)
+        return hit.astype(jnp.float32).astype(jnp.bfloat16)
+
+    def pack(p):
+        row = pl.multiple_of(p * 144, 16)
+        mw[p, :144] = mt_ref[0, pl.ds(row, 144), :]
+        mw[p, 144:] = mt_ref[1, pl.ds(row, 128), :]
+        tail = mt_ref[1, pl.ds(pl.multiple_of(row + 128, 16), 16), :]
+        for half in range(2):
+            lines = slice(half * 128, half * 128 + 128)
+            placed = lax.dot_general(
+                tail,
+                spare(half * 8),
+                (((0,), (0,)), ((), ())),
+                preferred_element_type=jnp.float32,
+            )
+            mw[p, lines] = (mw[p, lines].astype(jnp.float32) + placed).astype(jnp.bfloat16)
+        return mw.at[p]
+
+    def unpack(p, h):
+        taken = lax.dot_general(
+            spare(0),
+            mbuf[p, h, :256],
+            (((1,), (1,)), ((), ())),
+            preferred_element_type=jnp.float32,
+        )
+        nb[p, h, 0] = mbuf[p, h, :144]
+        nb[p, h, 1, :128] = mbuf[p, h, 144:]
+        nb[p, h, 1, 128:] = jnp.concatenate(
+            [taken[:8, :128], taken[:8, 128:]], axis=0
+        ).astype(jnp.bfloat16)
+
+    for dz in (1, 7, 2, 6, 3, 5, 4):
+        remote(amp_ref, abuf.at[chip, core, pair], a_sem.at[0], a_sem.at[1], z_to(dz)).start()
+
+    def send_block(i):
+        p = pair_to(PAIR_STEPS[i])
+        remote(pack(p), mbuf.at[pair, core], m_send, m_recv.at[i], (p, aux)).start()
+
+    for i in range(NEAR):
+        send_block(i)
+    remote(pack(pair), mbuf.at[pair, core], f_send, f_recv.at[15], partner).start()
+    for load in loads[2:8]:
         load.wait()
     lane = lax.broadcasted_iota(jnp.int32, (1, 128), 1)
     near_row = jnp.zeros((1, 128), jnp.int32)
@@ -178,43 +256,11 @@
     wgt_ref[...] = weight_row
     nbuf[pair] = near_row
     wbuf[pair] = weight_row
-    slot_row = lax.broadcasted_iota(jnp.int32, (16, 120), 0)
-    slot_col = lax.broadcasted_iota(jnp.int32, (16, 120), 1)
-    pick = ((slot_row < 15) & (slot_col == chip * 15 + slot_row)).astype(jnp.float32)
-    pick16 = pick.astype(jnp.bfloat16)
-    amp_ref[...] = jnp.zeros_like(amp_ref)
-    for s in range(2):
-        rows = jnp.dot(pick16, inamp[core, s], preferred_element_type=jnp.float32)
-        amp_ref[:, s * 128 : s * 128 + 120] = rows.astype(jnp.bfloat16)
-    abuf[chip, core, pair] = amp_ref[...]
-    loads[0].wait()
-    place_row = lax.broadcasted_iota(jnp.int32, (128, 120), 0)
-    place_col = lax.broadcasted_iota(jnp.int32, (128, 120), 1)
-    fill = lax.rem(place_row, 16)
-    source = place_row // 16 * 15 + fill
-    for c in range(2):
-        keep = (fill < 15) & (source == place_col) & (place_col < rank_ref[c])
-        place = keep.astype(jnp.float32).astype(jnp.bfloat16)
-        for t in range(9):
-            cols = pl.ds(t * 256, 256)
-            moved = jnp.dot(place, pbuf[c, :, cols], preferred_element_type=jnp.float32)
-            mt_ref[c, cols, :] = moved.astype(jnp.bfloat16).T
-    pl.semaphore_wait(barrier, 28)
-
-    def m_rows(p):
-        return mt_ref.at[:, pl.ds(pl.multiple_of(p * 144, 16), 144), :]
-
-    for dz in (1, 7, 2, 6, 3, 5, 4):
-        remote(amp_ref, abuf.at[chip, core, pair], a_sem.at[0], a_sem.at[1], z_to(dz)).start()
     for i, step in enumerate(PAIR_STEPS):
         to = (pair_to(step), aux)
         remote(nbr_ref, nbuf.at[pair], n_sem.at[0], n_sem.at[1], to).start()
         remote(wgt_ref, wbuf.at[pair], w_sem.at[0], w_sem.at[1], to).start()
-    for i, step in enumerate(PAIR_STEPS):
-        p = pair_to(step)
-        remote(m_rows(p), mbuf.at[pair, core], m_send, m_recv.at[i], (p, aux)).start()
-    remote(m_rows(pair), mbuf.at[pair, core], f_send, f_recv.at[15], partner).start()
-    mbuf[pair, core] = mt_ref[:, pl.ds(pl.multiple_of(pair * 144, 16), 144), :]
+    nb[pair, core] = mt_ref[:, pl.ds(pl.multiple_of(pair * 144, 16), 144), :]
     diag[...] = jnp.zeros_like(diag)
     own_row = lax.broadcasted_iota(jnp.int32, (8, 120), 0) + chip * 15 + core * 7
     own = (lax.broadcasted_iota(jnp.int32, (8, 120), 1) == own_row).astype(jnp.float32)
@@ -236,20 +282,22 @@
         block = mbuf.at[p, core]
         remote(block, block, m_send, m_recv.at[i], (p, aux)).wait_recv()
         remote(block, block, f_send, f_recv.at[i], partner).start()
+        unpack(p, core)
 
     def relayed(i):
         p = pair if i == 15 else pair_from(PAIR_STEPS[i])
         block = mbuf.at[p, other]
         remote(block, block, f_send, f_recv.at[i], partner).wait_recv()
+        unpack(p, other)
         for h in range(2):
-            mtr[p, h] = mbuf[p, h, core].T
+            mtr[p, h] = nb[p, h, core].T
         return p
 
     def project(p):
         for c in range(2):
             matrix = abuf[:, c, p].reshape(128, 256)
             for h in range(2):
-                block = jnp.dot(mbuf[p, h, c], matrix, preferred_element_type=jnp.float32)
+                block = jnp.dot(nb[p, h, c], matrix, preferred_element_type=jnp.float32)
                 proj[2 * p + c, h] = block.astype(jnp.bfloat16).astype(jnp.float32)
 
     def column(xx):
@@ -258,24 +306,24 @@
     def rows_of(yy, cc):
         return abuf.at[pl.ds(yy * 2, 2), cc]
 
-    relayed(15)
-    relay_block(0)
-    relay_block(1)
     arrived(abuf.at[0, 0, pl.ds(0, 7)], a_sem, partner)
     for d in RING:
         remote(column(x), column(x), b_sem.at[0], b_sem.at[1], x_to(d)).start()
     for d in RING:
         remote(column(x), column(x), y_sem.at[0], y_sem.at[1], y_to(d)).start()
-    relay_block(2)
+    for i in range(NEAR, 15):
+        send_block(i)
+    relayed(15)
+    relay_block(0)
+    relay_block(1)
     relayed(0)
-    relayed(1)
     arrived(abuf.at[pl.ds(0, 3), 0, pl.ds(0, 8)], b_sem, partner)
     for e in RING:
         for d in RING:
             xx = lax.rem(x + e, 4)
             remote(column(xx), column(xx), y_sem.at[0], y_sem.at[1], y_to(d)).start()
     remote(rows_of(y, core), rows_of(y, core), d_sem.at[0], d_sem.at[1], partner).start()
-    for i in range(3, EARLY):
+    for i in range(2, EARLY):
         relay_block(i)
         relayed(i - 1)
     arrived(abuf.at[pl.ds(0, 6), 0], y_sem, partner)
@@ -302,7 +350,9 @@
         project(relayed(i))
 
     def close(lo, zz):
-        p = lo * 8 + zz
+        odd = lax.rem(zz, 2)
+        target = (1 - odd) * lax.rem(8 - zz // 2, 8) + odd * ((zz + 1) // 2)
+        p = lo * 8 + target
         for h in range(2):
             total = jnp.zeros((144, 256), jnp.float32)
             for k in range(8):
@@ -313,9 +363,10 @@
         closed = jnp.dot(mtr[p, 0], coll[lo, 0], preferred_element_type=jnp.float32)
         closed = closed + jnp.dot(mtr[p, 1], coll[lo, 1], preferred_element_type=jnp.float32)
         closed = closed.astype(jnp.bfloat16).reshape(4, 2, 16, 256)
-        sa[:, :, lo, zz] = closed[:, :, :, :128]
+        q, j = zz // SPAN, lax.rem(zz, SPAN)
+        sa[:, q, :, lo, j] = closed[:, :, :, :128]
         for hi in range(2):
-            sb[hi, lo, :, zz] = closed[:, hi, :, 128:]
+            sb[hi, lo, q, :, j] = closed[:, hi, :, 128:]
 
     def close_both(zz, carry):
         close(0, zz)
@@ -330,26 +381,26 @@
         for i, d in enumerate(RING):
             yy, xx = lax.rem(y + d, 4), lax.rem(x + d, 4)
             remote(
-                sa.at[yy, :, :, span(q)],
-                ra.at[i, :, :, span(q)],
+                sa.at[yy, q],
+                ra.at[i, q],
                 r_send.at[0],
                 r_recv.at[0, q],
                 y_to(d),
             ).start()
             remote(
-                sb.at[xx // 2, lax.rem(xx, 2), :, span(q)],
-                rb.at[i, :, span(q)],
+                sb.at[xx // 2, lax.rem(xx, 2), q],
+                rb.at[i, q],
                 r_send.at[1],
                 r_recv.at[1, q],
                 x_to(d),
             ).start()
 
     def first_sum(q):
-        part = ra.at[:, :, :, span(q)]
+        part = ra.at[:, q]
         remote(part, part, r_send.at[0], r_recv.at[0, q], partner).wait_recv()
-        total = sa[y, :, :, span(q)].astype(jnp.float32)
+        total = sa[y, q].astype(jnp.float32)
         for i in range(3):
-            total = total + ra[i, :, :, span(q)].astype(jnp.float32)
+            total = total + ra[i, q].astype(jnp.float32)
         ta[:, :, span(q)] = total.astype(jnp.bfloat16)
         for i, d in enumerate(RING):
             xx = lax.rem(x + d, 4)
@@ -360,11 +411,11 @@
                 t_recv.at[0, q],
                 x_to(d),
             ).start()
-        part = rb.at[:, :, span(q)]
+        part = rb.at[:, q]
         remote(part, part, r_send.at[1], r_recv.at[1, q], partner).wait_recv()
-        total = sb[xhi, xlo, :, span(q)].astype(jnp.float32)
+        total = sb[xhi, xlo, q].astype(jnp.float32)
         for i in range(3):
-            total = total + rb[i, :, span(q)].astype(jnp.float32)
+            total = total + rb[i, q].astype(jnp.float32)
         tb[:, span(q)] = total.astype(jnp.bfloat16)
         for i, d in enumerate(RING):
             yy = lax.rem(y + d, 4)
@@ -391,33 +442,28 @@
             total = total + cb[i, span(q)].astype(jnp.float32)
         vbuf[span(q), 0, 1] = total[:, :8].astype(jnp.bfloat16)
         vbuf[span(q), 1, 1] = total[:, 7:15].astype(jnp.bfloat16)
-        for j in range(SPAN):
-            zz = q * SPAN + j
-            slot = lax.rem(zz - z + 8, 8)
+        for j in range(q * SPAN, (q + 1) * SPAN):
+            zz = Z_ORDER[j]
+            slot = lax.rem(zz - z + 8, 8) * 2 + core
             remote(
-                vbuf.at[zz, other],
-                ubuf.at[slot * 2 + core],
-                u_sem.at[0],
-                u_sem.at[1],
-                at(x, y, zz, other),
+                vbuf.at[j, other], ubuf.at[slot], u_sem.at[0], u_sem.at[1], at(x, y, zz, other)
             ).start()
+
+            @pl.when(zz == z)
+            def _():
+                ubuf[core] = vbuf[j, core]
 
             @pl.when(zz != z)
             def _():
                 remote(
-                    vbuf.at[zz, core],
-                    ubuf.at[slot * 2 + core],
-                    u_sem.at[0],
-                    u_sem.at[1],
-                    at(x, y, zz, core),
+                    vbuf.at[j, core], ubuf.at[slot], u_sem.at[0], u_sem.at[1], at(x, y, zz, core)
                 ).start()
 
-    first_sum(0)
-    for q in range(1, GROUPS):
-        first_sum(q)
-        second_sum(q - 1)
-    second_sum(GROUPS - 1)
-    ubuf[core] = vbuf[z, core]
+    for q in range(GROUPS + LAG):
+        if q < GROUPS:
+            first_sum(q)
+        if q >= LAG:
+            second_sum(q - LAG)
     arrived(ubuf.at[pl.ds(0, 15)], u_sem, partner)
     for c in range(2):
         total = diag[c]
@@ -470,6 +516,8 @@
             pltpu.VMEM((1, 128), f32),
             pltpu.VMEM((2, 2, 8, 128), f32),
             pltpu.VMEM((4, 1024), f32),
+            pltpu.VMEM((16, 272, 128), bf16),
+            pltpu.VMEM((16, 2, 272, 128), bf16),
             pltpu.VMEM((16, 2, 2, 144, 128), bf16),
             pltpu.VMEM((8, 2, 16, 16, 256), bf16),
             pltpu.VMEM((16, 1, 128), i32),
@@ -479,10 +527,10 @@
             pltpu.VMEM((32, 2, 144, 256), f32),
             pltpu.VMEM((16, 2, 128, 144), bf16),
             pltpu.VMEM((2, 2, 144, 256), bf16),
-            pltpu.VMEM((4, 2, 2, 8, 16, 128), bf16),
-            pltpu.VMEM((2, 2, 4, 8, 16, 128), bf16),
-            pltpu.VMEM((3, 2, 2, 8, 16, 128), bf16),
-            pltpu.VMEM((3, 4, 8, 16, 128), bf16),
+            pltpu.VMEM((4, GROUPS, 2, 2, SPAN, 16, 128), bf16),
+            pltpu.VMEM((2, 2, GROUPS, 4, SPAN, 16, 128), bf16),
+            pltpu.VMEM((3, GROUPS, 2, 2, SPAN, 16, 128), bf16),
+            pltpu.VMEM((3, GROUPS, 4, SPAN, 16, 128), bf16),
             pltpu.VMEM((2, 2, 8, 16, 128), bf16),
             pltpu.VMEM((4, 8, 16, 128), bf16),
             pltpu.VMEM((3, 8, 16, 128), bf16),

time: 59 us -> 58.4 us (0.990)
  Pallas kernels: 57.6 us -> 57 us
    pallas_call x1, Pallas kernels: 57.6 us -> 57 us  [coupled_rows(): pl.pallas_call(kernel, out_shape=jax.ShapeDtypeStruct((2, 2, 900), f32),...]
where the time goes in v5:
time: 58.4 us; the launch traced here: 58.3 us
  Pallas kernels  57 us (98%)
  between operations  0.68 us (1%)
  other arithmetic  0.62 us (1%)
    pallas_call x1, Pallas kernels, coupled_rows(): pl.pallas_call(kernel, out_shape=jax.ShapeDtypeStruct((2, 2, 900), f32),...  57 us

profile of v5, /device:TPU:1, one launch (start us, length us, event | category | flops | bytes accessed | tf_op | source)
XLA Modules:
  0.0 58.3 jit_solution(15777883886207492973)
XLA Ops:
  0.0 0.0 copy-start
  0.7 57.0 %coupled_rows.1 = f32[2,2,900]{2,1,0:T(2,128)S(1)} custom-call(bf16[2,120,2304]{2,1,0:T(8,128)(2,1)} %panel_ref.1, bf16[2,2,120,120]{3,2,1,0:T(8,128)(2,1)} %amplitude_ref.1, f32[2,120]{1,0:T(2,128)} %energy_in.1, f32[64,64]{1,0:T(8,128)} %fock_in.1, f32[64]{0:T(128)} %occ_in.1, f32[1]{0:T(128)S(6)} %copy.11.freq_in, s32[2,32]{1,0:T(2,128)} %bitcast.1, ...), custom_call_target="tpu_custom_call" | custom-call | tf_op jit(solution)/shard_map/coupled_rows/pallas_call | solution.py:498
  57.7 0.0 copy-done
  57.7 0.6 %add.3 = f32[2,2,900]{2,1,0:T(2,128)} add(f32[2,2,900]{2,1,0:T(2,128)S(1)} %copy-done, f32[2,2,900]{2,1,0:T(2,128)S(1)} %coupled_rows.1) | non-fusion elementwise | flops 3600 | bytes 43200 | tf_op jit(solution)/shard_map/add | solution.py:576
Async XLA Ops:
  0.0 57.7 %copy-start = (f32[2,2,900]{2,1,0:T(2,128)S(1)}, f32[2,2,900]{2,1,0:T(2,128)}, u32[]{:S(2)}) copy-start(f32[2,2,900]{2,1,0:T(2,128)} %param.12) | copy-start | bytes 43204

commit v6 on v5

--- a/solution.py
+++ b/solution.py
@@ -10,11 +10,11 @@
 PAIR_STEPS = [(0, dz) for dz in (1, 7, 2, 6, 3, 5, 4)]
 PAIR_STEPS += [(1, dz) for dz in (0, 1, 7, 2, 6, 3, 5, 4)]
 NEAR = 7
-RING = (1, 3, 2)
+RING = (2, 1, 3)
 GROUPS = 4
 SPAN = 8 // GROUPS
 EARLY = 10
-LAG = 2
+LAG = 4
 Z_ORDER = (0, 1, 7, 2, 6, 3, 5, 4)
 
 

time: 58.4 us -> 58.4 us (level)
  no operation moved by 1% of the time
where the time goes in v6:
time: 58.4 us; the launch traced here: 58.3 us
  Pallas kernels  57 us (98%)
  between operations  0.68 us (1%)
  other arithmetic  0.62 us (1%)
    pallas_call x1, Pallas kernels, coupled_rows(): pl.pallas_call(kernel, out_shape=jax.ShapeDtypeStruct((2, 2, 900), f32),...  57 us

profile of v6, /device:TPU:1, one launch (start us, length us, event | category | flops | bytes accessed | tf_op | source)
XLA Modules:
  0.0 58.3 jit_solution(9502236179666120499)
XLA Ops:
  0.0 0.0 copy-start
  0.7 57.0 %coupled_rows.1 = f32[2,2,900]{2,1,0:T(2,128)S(1)} custom-call(bf16[2,120,2304]{2,1,0:T(8,128)(2,1)} %panel_ref.1, bf16[2,2,120,120]{3,2,1,0:T(8,128)(2,1)} %amplitude_ref.1, f32[2,120]{1,0:T(2,128)} %energy_in.1, f32[64,64]{1,0:T(8,128)} %fock_in.1, f32[64]{0:T(128)} %occ_in.1, f32[1]{0:T(128)S(6)} %copy.11.freq_in, s32[2,32]{1,0:T(2,128)} %bitcast.1, ...), custom_call_target="tpu_custom_call" | custom-call | tf_op jit(solution)/shard_map/coupled_rows/pallas_call | solution.py:498
  57.7 0.0 copy-done
  57.7 0.6 %add.3 = f32[2,2,900]{2,1,0:T(2,128)} add(f32[2,2,900]{2,1,0:T(2,128)S(1)} %copy-done, f32[2,2,900]{2,1,0:T(2,128)S(1)} %coupled_rows.1) | non-fusion elementwise | flops 3600 | bytes 43200 | tf_op jit(solution)/shard_map/add | solution.py:576
Async XLA Ops:
  0.0 57.7 %copy-start = (f32[2,2,900]{2,1,0:T(2,128)S(1)}, f32[2,2,900]{2,1,0:T(2,128)}, u32[]{:S(2)}) copy-start(f32[2,2,900]{2,1,0:T(2,128)} %param.12) | copy-start | bytes 43204
